TPU v7x, 256 devices: a whole 4x4x8 slice. The times are simulated.
256 devices in a mesh: tm: 64 (over x, z, core), env: 4 (over y).
Axes of the slice: x: 4, y: 4, z: 8, core: 2. Of those that a mesh axis runs over, the one named last changes fastest.
Arguments:
- init_state: float32 [70, 1024], P(None, 'env'), may hold values from -6 to 6
- torque: float32 [256, 35, 1024], P('tm', None, 'env'), may hold values from -192 to 192
- contact: int32 [256, 1024], P('tm', 'env'), may hold values 0 or 1
- mass_inverse: float32 [128, 35, 35], P('tm'), may hold values from -0.014 to 1.5, as said below
- stiffness: float32 [35], replicated, may hold values from 10 to 100
- damping: float32 [35], replicated, may hold values from 0.5 to 5
- gravity: float32 [35], replicated, may hold values from 1 to 10
- contact_stiffness: float32 [35], replicated, may hold values from 20 to 100
- contact_damping: float32 [35], replicated, may hold values from 0.5 to 3
Outputs:
- final_states: float32 [128, 70, 1024], P('tm', None, 'env')
- corrections: float32 [3, 1024], P(None, 'env')
Inputs may be any that keep to these rules, and one draw needn't show every extreme that they name: `mass_inverse`: each matrix is symmetric, and each diagonal entry exceeds the sum of the magnitudes of the other entries of its row.
All inputs are finite; a program needn't handle non-finite values. No bound on the sum of `contact` on one device may be relied on, other than what follows from the above.
Results may differ from a plain program's by a relative error of at most 0.00025.
Values sent between devices are 32-bit elements; how exact they have to be, the bound alone decides.
A program may use at most 64 MiB of HBM per device.

v0:
```python
import jax
import jax.numpy as jnp
from jax import lax
from jax.sharding import Mesh
from jax.sharding import PartitionSpec as P

DOF = 35
HS = 2
SUB = 32
ITERS = 3
TM = ("tm_0", "tm_1", "tm_2")


step_length = 0.05


def sent_to_all(value, axis):
    copies = jnp.broadcast_to(value, (lax.axis_size(axis), *value.shape))
    return lax.all_to_all(copies, axis, split_axis=0, concat_axis=0, tiled=True)


def of_everyone(value, axis):
    return sent_to_all(value, axis).sum(axis=0)


def neutral_like(value, identity):
    return jax.tree.map(
        lambda part, zero: jnp.zeros_like(part) + jnp.asarray(zero, part.dtype), value, identity
    )


def prefix_by_axis(value, axes, combine, identity):
    before = start = neutral_like(value, identity)
    running = value
    for axis in reversed(axes):
        count, index = (lax.axis_size(axis), lax.axis_index(axis))
        pieces = jax.tree.map(lambda part: lax.all_gather(part, axis), running)
        inside, running = (start, start)
        for k in range(count):
            passed = k < index
            running = combine(running, jax.tree.map(lambda part: part[k], pieces))
            inside = jax.tree.map(lambda new, old: jnp.where(passed, new, old), running, inside)
        before = combine(inside, before)
    return before


def taken_together(value, axis):
    return sent_to_all(value, axis).max(axis=0)


def exact_dot(left, right):
    return jnp.dot(left, right, precision=lax.Precision.HIGHEST, preferred_element_type=jnp.float32)


def coarse_one(state_now, torque_steps, mean_steps, inverse, params):
    stiffness, damping, gravity, contact_stiffness, contact_damping = params
    joint_pos = state_now[:DOF]
    joint_vel = state_now[DOF:]
    for step_pos in range(HS):
        spring = (stiffness + gravity + mean_steps[step_pos] * contact_stiffness)[:, None]
        friction = (damping + mean_steps[step_pos] * contact_damping)[:, None]
        force = torque_steps[step_pos] - spring * joint_pos - friction * joint_vel
        joint_vel = joint_vel + step_length * exact_dot(inverse, force)
        joint_pos = joint_pos + step_length * joint_vel
    return jnp.concatenate([joint_pos, joint_vel], axis=0)


def fine_one(state_now, torque_steps, contact_steps, inverse, params):
    stiffness, damping, gravity, contact_stiffness, contact_damping = params
    fine_dt = step_length / SUB
    joint_pair = (state_now[:DOF], state_now[DOF:])
    for step_pos in range(HS):
        torque_here = torque_steps[step_pos]
        contact_here = contact_steps[step_pos][None, :]

        def substep(counter, pair_now):
            joint_pos, joint_vel = pair_now
            force = (
                torque_here
                - stiffness[:, None] * joint_pos
                - damping[:, None] * joint_vel
                - gravity[:, None] * jnp.sin(joint_pos)
                - contact_here
                * (contact_stiffness[:, None] * joint_pos + contact_damping[:, None] * joint_vel)
            )
            joint_vel = joint_vel + fine_dt * exact_dot(inverse, force)
            joint_pos = joint_pos + fine_dt * joint_vel
            return (joint_pos, joint_vel)

        joint_pair = lax.fori_loop(0, SUB, substep, joint_pair, unroll=min(8, SUB))
    return jnp.concatenate([joint_pair[0], joint_pair[1]], axis=0)


def compose(former, latter):
    return (exact_dot(latter[0], former[0]), exact_dot(latter[0], former[1]) + latter[1])


def shards(
    init_state,
    torque,
    contact,
    mass_inverse,
    stiffness,
    damping,
    gravity,
    contact_stiffness,
    contact_damping,
):
    params = (stiffness, damping, gravity, contact_stiffness, contact_damping)
    local_slices = mass_inverse.shape[0]
    env_local = init_state.shape[1]
    state_rows = init_state.shape[0]
    torque_steps = torque.reshape(local_slices, HS, DOF, env_local)
    contact_float = contact.astype(jnp.float32)
    contact_steps = contact_float.reshape(local_slices, HS, env_local)
    totals = of_everyone(jnp.sum(contact_float, axis=1), "env")
    mean_steps = (totals / (env_local * lax.axis_size("env"))).reshape(local_slices, HS)
    eye_state = jnp.eye(state_rows, dtype=jnp.float32)
    zero_shift = jnp.zeros((state_rows, env_local), jnp.float32)
    no_force = jnp.zeros((local_slices, HS, DOF, 1), jnp.float32)
    step_maps = jax.vmap(coarse_one, in_axes=(None, 0, 0, 0, None))(
        eye_state, no_force, mean_steps, mass_inverse, params
    )
    coarse_free = jax.vmap(coarse_one, in_axes=(0, 0, 0, 0, None))(
        jnp.zeros((local_slices, state_rows, env_local), jnp.float32),
        torque_steps,
        mean_steps,
        mass_inverse,
        params,
    )
    device_map = eye_state
    for slot_pos in range(local_slices):
        device_map = exact_dot(step_maps[slot_pos], device_map)

    def sweep(offsets):
        local_shift = zero_shift
        for slot_pos in range(local_slices):
            local_shift = exact_dot(step_maps[slot_pos], local_shift) + offsets[slot_pos]
        prefix_map, prefix_shift = prefix_by_axis(
            (device_map, local_shift), TM, compose, (eye_state, zero_shift)
        )
        entry = exact_dot(prefix_map, init_state) + prefix_shift
        start_list = []
        end_list = []
        current = entry
        for slot_pos in range(local_slices):
            start_list.append(current)
            current = exact_dot(step_maps[slot_pos], current) + offsets[slot_pos]
            end_list.append(current)
        return (jnp.stack(start_list), jnp.stack(end_list))

    starts, ends = sweep(coarse_free)
    fine_all = jax.vmap(fine_one, in_axes=(0, 0, 0, 0, None))
    records = []
    for iteration in range(ITERS):
        fine_end = fine_all(starts, torque_steps, contact_steps, mass_inverse, params)
        jumps = fine_end - jnp.einsum(
            "sij,sje->sie", step_maps, starts, precision=lax.Precision.HIGHEST
        )
        new_starts, new_ends = sweep(jumps)
        local_max = jnp.max(jnp.sqrt(jnp.sum((new_ends - ends) ** 2, axis=1)), axis=0)
        records.append(local_max)
        starts, ends = (new_starts, new_ends)
    corrections = jnp.stack(records)
    corrections = taken_together(corrections, TM)
    return (ends, corrections)


def solution(mesh):
    torus = Mesh(mesh.devices.reshape(4, 8, 2, mesh.shape["env"]), ("tm_0", "tm_1", "tm_2", "env"))
    return jax.shard_map(
        shards,
        mesh=torus,
        in_specs=(
            P(None, "env"),
            P(TM, None, "env"),
            P(TM, "env"),
            P(TM, None, None),
            P(),
            P(),
            P(),
            P(),
            P(),
        ),
        out_specs=(P(TM, None, "env"), P(None, "env")),
        check_vma=False,
    )
```

profile of v0, /device:TPU:1, one launch (start us, length us, event | category | flops | bytes accessed | tf_op | source)
XLA Modules:
  0.0 363.3 jit_solution(5527427069862304610)
XLA Ops:
  0.6 0.8 convert_reduce_fusion
  1.5 0.6 broadcast_in_dim.6
  2.1 5.0 %all-to-all-start = ((f32[4,1,4]{2,1,0:T(1,128)}), f32[4,1,4]{2,1,0:T(1,128)S(1)}, u32[]{:S(2)}, u32[]{:S(2)}) async-start(f32[4,1,4]{2,1,0:T(1,128)} %broadcast_in_dim.6), calls=%async_computation | async-start | bytes 4096 | tf_op jit(solution)/shard_map/all_to_all | solution.py:19
  7.1 0.7 copy-done.8
  7.9 0.7 copy-done.6
  8.9 0.6 copy-done.4
  9.6 1.5 all-to-all-done
  11.5 0.6 copy-done.1
  13.2 4.1 %all-gather.15 = f32[2,70,70]{2,1,0:T(8,128)S(1)} all-gather(f32[1,70,70]{2,1,0:T(8,128)S(1)} %convolution_bitcast_fusion), channel_id=2, replica_groups=mesh['tm_0'=4,'tm_1'=8,'tm_2'=2,'env'=4] {'tm_2'}, dimensions={0}, use_global_device_ids=true | all-gather | bytes 58800 | tf_op jit(solution)/shard_map/all_gather | solution.py:37
  18.0 22.1 %all-gather.16 = f32[8,70,70]{2,1,0:T(8,128)S(1)} all-gather(f32[1,70,70]{2,1,0:T(8,128)S(1)} %bitcast.1051), channel_id=3, replica_groups=mesh['tm_0'=4,'tm_1'=8,'tm_2'=2,'env'=4] {'tm_1'}, dimensions={0}, use_global_device_ids=true | all-gather | bytes 176400 | tf_op jit(solution)/shard_map/all_gather | solution.py:37
  42.0 9.5 %all-gather.17 = f32[4,70,70]{2,1,0:T(8,128)S(1)} all-gather(f32[1,70,70]{2,1,0:T(8,128)S(1)} %bitcast.1050), channel_id=4, replica_groups=mesh['tm_0'=4,'tm_1'=8,'tm_2'=2,'env'=4] {'tm_0'}, dimensions={0}, use_global_device_ids=true | all-gather | bytes 98000 | tf_op jit(solution)/shard_map/all_gather | solution.py:37
  53.0 10.7 %all-gather.18 = f32[2,70,256]{2,1,0:T(8,128)S(1)} all-gather(f32[1,70,256]{2,1,0:T(8,128)S(1)} %fusion.1029), channel_id=5, replica_groups=mesh['tm_0'=4,'tm_1'=8,'tm_2'=2,'env'=4] {'tm_2'}, dimensions={0}, use_global_device_ids=true | all-gather | bytes 215040 | tf_op jit(solution)/shard_map/all_gather | solution.py:37
  64.3 19.9 %all-gather.19 = f32[8,70,256]{2,1,0:T(8,128)S(1)} all-gather(f32[1,70,256]{2,1,0:T(8,128)S(1)} %bitcast.1047), channel_id=6, replica_groups=mesh['tm_0'=4,'tm_1'=8,'tm_2'=2,'env'=4] {'tm_1'}, dimensions={0}, use_global_device_ids=true | all-gather | bytes 645120 | tf_op jit(solution)/shard_map/all_gather | solution.py:37
  86.4 9.6 %all-gather.20 = f32[4,70,256]{2,1,0:T(8,128)S(1)} all-gather(f32[1,70,256]{2,1,0:T(8,128)S(1)} %bitcast.1041), channel_id=7, replica_groups=mesh['tm_0'=4,'tm_1'=8,'tm_2'=2,'env'=4] {'tm_0'}, dimensions={0}, use_global_device_ids=true | all-gather | bytes 358400 | tf_op jit(solution)/shard_map/all_gather | solution.py:37
  98.1 17.2 %while.72 = (s32[]{:T(128)}, f32[2,35,256]{2,1,0:T(8,128)S(1)}, f32[2,35,256]{2,1,0:T(8,128)S(1)}, f32[35]{0:T(128)S(1)}, f32[2,35,256]{2,1,0:T(8,128)S(1)}, /*i...) while((s32[]{:T(128)}, f32[2,35,256]{2,1,0:T(8,128)S(1)}, ...), condition=%wide.region_3.4_spmd, body=%wide.region_2.3_spmd.sunk | while | flops 62504960 | bytes 2680981 | solution.py:90
  98.7 0.5 multiply_add_fusion.107
  99.7 0.5 multiply_add_fusion.108
  101.9 0.5 multiply_add_fusion.110
  102.9 0.5 multiply_add_fusion.107
  104.0 0.5 multiply_add_fusion.108
  106.2 0.5 multiply_add_fusion.110
  107.2 0.5 multiply_add_fusion.107
  115.3 17.2 %while.73 = (s32[]{:T(128)}, f32[2,35,256]{2,1,0:T(8,128)S(1)}, f32[2,35,256]{2,1,0:T(8,128)S(1)}, f32[35]{0:T(128)S(1)}, f32[2,35,256]{2,1,0:T(8,128)S(1)}, /*i...) while((s32[]{:T(128)}, f32[2,35,256]{2,1,0:T(8,128)S(1)}, ...), condition=%wide.region_5.6_spmd, body=%wide.region_4.5_spmd.sunk | while | flops 62504960 | bytes 2680981 | solution.py:90
  133.0 10.3 %all-gather.21 = f32[2,70,256]{2,1,0:T(8,128)S(1)} all-gather(f32[1,70,256]{2,1,0:T(8,128)S(1)} %fusion.1025), channel_id=8, replica_groups=mesh['tm_0'=4,'tm_1'=8,'tm_2'=2,'env'=4] {'tm_2'}, dimensions={0}, use_global_device_ids=true | all-gather | bytes 215040 | tf_op jit(solution)/shard_map/all_gather | solution.py:37
  143.5 19.6 %all-gather.22 = f32[8,70,256]{2,1,0:T(8,128)S(1)} all-gather(f32[1,70,256]{2,1,0:T(8,128)S(1)} %bitcast.1048), channel_id=9, replica_groups=mesh['tm_0'=4,'tm_1'=8,'tm_2'=2,'env'=4] {'tm_1'}, dimensions={0}, use_global_device_ids=true | all-gather | bytes 645120 | tf_op jit(solution)/shard_map/all_gather | solution.py:37
  164.8 9.6 %all-gather.23 = f32[4,70,256]{2,1,0:T(8,128)S(1)} all-gather(f32[1,70,256]{2,1,0:T(8,128)S(1)} %bitcast.1044), channel_id=10, replica_groups=mesh['tm_0'=4,'tm_1'=8,'tm_2'=2,'env'=4] {'tm_0'}, dimensions={0}, use_global_device_ids=true | all-gather | bytes 358400 | tf_op jit(solution)/shard_map/all_gather | solution.py:37
  175.9 17.2 %while.74 = (s32[]{:T(128)}, f32[2,35,256]{2,1,0:T(8,128)S(1)}, f32[2,35,256]{2,1,0:T(8,128)S(1)}, f32[35]{0:T(128)S(1)}, f32[2,35,256]{2,1,0:T(8,128)S(1)}, /*i...) while((s32[]{:T(128)}, f32[2,35,256]{2,1,0:T(8,128)S(1)}, ...), condition=%wide.region_7.8_spmd, body=%wide.region_6.7_spmd.sunk | while | flops 62504960 | bytes 2680981 | solution.py:90
  180.8 0.5 multiply_add_fusion.115
  181.8 0.5 multiply_add_fusion.116
  193.1 17.2 %while.75 = (s32[]{:T(128)}, f32[2,35,256]{2,1,0:T(8,128)S(1)}, f32[2,35,256]{2,1,0:T(8,128)S(1)}, f32[35]{0:T(128)S(1)}, f32[2,35,256]{2,1,0:T(8,128)S(1)}, /*i...) while((s32[]{:T(128)}, f32[2,35,256]{2,1,0:T(8,128)S(1)}, ...), condition=%wide.region_9.10_spmd, body=%wide.region_8.9_spmd.sunk | while | flops 62504960 | bytes 2680981 | solution.py:90
  210.8 11.0 %all-gather.24 = f32[2,70,256]{2,1,0:T(8,128)S(1)} all-gather(f32[1,70,256]{2,1,0:T(8,128)S(1)} %fusion.1021), channel_id=11, replica_groups=mesh['tm_0'=4,'tm_1'=8,'tm_2'=2,'env'=4] {'tm_2'}, dimensions={0}, use_global_device_ids=true | all-gather | bytes 215040 | tf_op jit(solution)/shard_map/all_gather | solution.py:37
  222.0 19.5 %all-gather.25 = f32[8,70,256]{2,1,0:T(8,128)S(1)} all-gather(f32[1,70,256]{2,1,0:T(8,128)S(1)} %bitcast.1049), channel_id=12, replica_groups=mesh['tm_0'=4,'tm_1'=8,'tm_2'=2,'env'=4] {'tm_1'}, dimensions={0}, use_global_device_ids=true | all-gather | bytes 645120 | tf_op jit(solution)/shard_map/all_gather | solution.py:37
  243.2 9.7 %all-gather.26 = f32[4,70,256]{2,1,0:T(8,128)S(1)} all-gather(f32[1,70,256]{2,1,0:T(8,128)S(1)} %bitcast.1045), channel_id=13, replica_groups=mesh['tm_0'=4,'tm_1'=8,'tm_2'=2,'env'=4] {'tm_0'}, dimensions={0}, use_global_device_ids=true | all-gather | bytes 358400 | tf_op jit(solution)/shard_map/all_gather | solution.py:37
  254.4 17.2 %while.76 = (s32[]{:T(128)}, f32[2,35,256]{2,1,0:T(8,128)S(1)}, f32[2,35,256]{2,1,0:T(8,128)S(1)}, f32[35]{0:T(128)S(1)}, f32[2,35,256]{2,1,0:T(8,128)S(1)}, /*i...) while((s32[]{:T(128)}, f32[2,35,256]{2,1,0:T(8,128)S(1)}, ...), condition=%wide.region_11.12_spmd, body=%wide.region_10.11_spmd.sunk | while | flops 62504960 | bytes 2680981 | solution.py:90
  255.0 0.5 multiply_add_fusion.123
  256.0 0.5 multiply_add_fusion.124
  259.3 0.5 multiply_add_fusion.123
  267.8 0.5 multiply_add_fusion.123
  268.9 0.5 multiply_add_fusion.124
  271.6 17.1 %while.77 = (s32[]{:T(128)}, f32[2,35,256]{2,1,0:T(8,128)S(1)}, f32[2,35,256]{2,1,0:T(8,128)S(1)}, f32[35]{0:T(128)S(1)}, f32[2,35,256]{2,1,0:T(8,128)S(1)}, /*i...) while((s32[]{:T(128)}, f32[2,35,256]{2,1,0:T(8,128)S(1)}, ...), condition=%wide.region_13.14_spmd, body=%wide.region_12.13_spmd.sunk | while | flops 62504960 | bytes 2680981 | solution.py:90
  289.3 10.9 %all-gather.27 = f32[2,70,256]{2,1,0:T(8,128)S(1)} all-gather(f32[1,70,256]{2,1,0:T(8,128)S(1)} %fusion.1017), channel_id=14, replica_groups=mesh['tm_0'=4,'tm_1'=8,'tm_2'=2,'env'=4] {'tm_2'}, dimensions={0}, use_global_device_ids=true | all-gather | bytes 215040 | tf_op jit(solution)/shard_map/all_gather | solution.py:37
  300.4 19.4 %all-gather.28 = f32[8,70,256]{2,1,0:T(8,128)S(1)} all-gather(f32[1,70,256]{2,1,0:T(8,128)S(1)} %bitcast.1046), channel_id=15, replica_groups=mesh['tm_0'=4,'tm_1'=8,'tm_2'=2,'env'=4] {'tm_1'}, dimensions={0}, use_global_device_ids=true | all-gather | bytes 645120 | tf_op jit(solution)/shard_map/all_gather | solution.py:37
  321.5 9.7 %all-gather.29 = f32[4,70,256]{2,1,0:T(8,128)S(1)} all-gather(f32[1,70,256]{2,1,0:T(8,128)S(1)} %bitcast.1042), channel_id=16, replica_groups=mesh['tm_0'=4,'tm_1'=8,'tm_2'=2,'env'=4] {'tm_0'}, dimensions={0}, use_global_device_ids=true | all-gather | bytes 358400 | tf_op jit(solution)/shard_map/all_gather | solution.py:37
  332.8 0.7 broadcast_in_dim.8
  333.6 16.7 %all-to-all-start.1 = ((f32[64,3,256]{2,1,0:T(4,128)}), f32[64,3,256]{2,1,0:T(4,128)S(1)}, u32[]{:S(2)}, u32[]{:S(2)}) async-start(f32[64,3,256]{2,1,0:T(4,128)} %broadcast_in_dim.8), calls=%async_computation.1 | async-start | bytes 524288 | tf_op jit(solution)/shard_map/all_to_all | solution.py:19
  350.2 0.7 copy.119
  351.0 11.2 %all-to-all-done.1 = f32[64,3,256]{2,1,0:T(4,128)S(1)} async-done(((f32[64,3,256]{2,1,0:T(4,128)}), f32[64,3,256]{2,1,0:T(4,128)S(1)}, u32[]{:S(2)}, u32[]{:S(2)}) %all-to-all-start.1) | async-done | bytes 196640 | tf_op jit(solution)/shard_map/all_to_all | solution.py:19
  362.2 0.7 reduce_max.39
  (321 shorter events, 115.5 us)
Async XLA Ops:
  0.6 96.6 %copy-start = (f32[70,256]{1,0:T(8,128)S(1)}, f32[70,256]{1,0:T(8,128)}, u32[]{:S(2)}) copy-start(f32[70,256]{1,0:T(8,128)} %param.21) | copy-start | bytes 215044
  2.1 9.1 %all-to-all-start = ((f32[4,1,4]{2,1,0:T(1,128)}), f32[4,1,4]{2,1,0:T(1,128)S(1)}, u32[]{:S(2)}, u32[]{:S(2)}) async-start(f32[4,1,4]{2,1,0:T(1,128)} %broadcast_in_dim.6), calls=%async_computation | async-start | bytes 4096 | tf_op jit(solution)/shard_map/all_to_all | solution.py:19
  7.1 0.7 copy-start.8
  7.1 1.5 copy-start.7
  7.8 0.8 copy-start.6
  8.9 0.7 copy-start.4
  8.9 0.7 copy-start.5
  11.4 0.7 copy-start.1
  11.4 0.7 copy-start.2
  11.4 0.7 copy-start.3
  333.6 28.6 %all-to-all-start.1 = ((f32[64,3,256]{2,1,0:T(4,128)}), f32[64,3,256]{2,1,0:T(4,128)S(1)}, u32[]{:S(2)}, u32[]{:S(2)}) async-start(f32[64,3,256]{2,1,0:T(4,128)} %broadcast_in_dim.8), calls=%async_computation.1 | async-start | bytes 524288 | tf_op jit(solution)/shard_map/all_to_all | solution.py:19
where the time goes:
time: 368 us; the launch traced here: 363 us
  blocking collectives  196 us (53%)
  matrix products  122 us (33%)
  starting transfers between devices  21.7 us (6%)
  waiting for transfers between devices  12.8 us (3%)
  local copies, waits for them, and re-layouts  5.6 us (2%)
    all_gather x15, blocking collectives, prefix_by_axis(): pieces = jax.tree.map(lambda part: lax.all_gather(part, axis), running)  196 us
    dot_general x288, matrix products, exact_dot(): jnp.dot(left, right, precision=lax.Precision.HIGHEST, preferred_element_t...  121 us
    all_to_all x2, starting transfers between devices, sent_to_all(): return lax.all_to_all(copies, axis, split_axis=0, concat_axis=0, tiled=True)  21.7 us
    all_to_all x2, waiting for transfers between devices, sent_to_all(): return lax.all_to_all(copies, axis, split_axis=0, concat_axis=0, tiled=True)  12.8 us
  transfers between devices with their start and end apart: 2, of which 2 were waited for; matrix products, arithmetic and copies ran while one was open for 0% of the time, Pallas kernels for 0%

commit v1 on v0

v1 whole, which is shorter than its diff:
```python
import math

import jax
import jax.numpy as jnp
import numpy as np
from jax import lax
from jax.experimental import pallas as pl
from jax.experimental.pallas import tpu as pltpu
from jax.sharding import Mesh
from jax.sharding import PartitionSpec as P

DOF = 35
STATE = 70
SUB = 32
ITERS = 3
SWEEPS = ITERS + 1
NX, NZ, NC, NE = 4, 8, 2, 4
GROUP = NZ * NC
ENV = 256
BLOCK = ENV // GROUP
LANES = 128
HALF = 64
ROWS = 72
DT = 0.05
H = DT / SUB
TWO_PI = 2.0 * math.pi
MAGIC = 12582912.0
F32 = jnp.float32
BF16 = jnp.bfloat16
MESH = pl.DeviceIdType.MESH
HIGHEST = lax.Precision.HIGHEST
TM = ("x", "z", "c")
Z_OFFSETS = (4, 3, 5, 2, 6, 1, 7, 0)


def sine_coefficients(terms):
    x = np.cos(np.linspace(0, np.pi, 4001)) * 0.25 + 0.25
    x = x[x > 1e-4]
    basis = np.stack([x ** (2 * i + 1) for i in range(terms)], 1)
    target = np.sin(2 * np.pi * x)
    weight = np.ones_like(x)
    for _ in range(200):
        c = np.linalg.lstsq(basis * weight[:, None], target * weight, rcond=None)[0]
        weight = weight * (1e-12 + np.abs(basis @ c - target)) ** 0.1
        weight /= weight.mean()
    return [float(np.float32(v)) for v in c]


SINE = sine_coefficients(6)


def selectors():
    pick = np.zeros((2, 2 * LANES, LANES), np.float32)
    for s in range(2):
        for i in range(DOF):
            pick[s, HALF * s + i, i] = 1.0
            pick[s, LANES + HALF * s + i, DOF + i] = 1.0
    return pick


PICK = selectors()


def split(x):
    hi = x.astype(BF16)
    lo = (x - hi.astype(F32)).astype(BF16)
    return hi, lo


def dot(a, b):
    return jnp.dot(a, b, preferred_element_type=F32)


def exact(a, b):
    return jnp.dot(a, b, precision=HIGHEST, preferred_element_type=F32)


def exact_ta(a, b):
    return lax.dot_general(a, b, (((0,), (0,)), ((), ())), precision=HIGHEST, preferred_element_type=F32)


def exact_tb(a, b):
    return lax.dot_general(a, b, (((1,), (1,)), ((), ())), precision=HIGHEST, preferred_element_type=F32)


def wide(x, weights):
    hi, lo = split(x)
    return dot(hi, weights[0]) + dot(lo, weights[0]) + dot(hi, weights[1])


def put_pair(ref, value):
    hi, lo = split(value)
    ref[0] = hi
    ref[1] = lo


def put_side(ref, index, value):
    hi, lo = split(value)
    ref[index, :, 0:LANES] = hi
    ref[index, :, LANES:] = lo


def small(x, weights):
    hi, lo = split(x)
    out = dot(jnp.concatenate([hi, lo], axis=0), weights)
    both = out[:, 0:LANES] + out[:, LANES:]
    return both[0:BLOCK] + both[BLOCK:]


def body(
    init_ref, torque_ref, contact_ref, block_ref, par_ref, pick_ref,
    final_ref, corr_out_ref,
    flip, tau, kk, dd, q_ref, v_ref, init_t, nfine, free, jall, start, gee, ends, jshift,
    mf_w, zf_w, ze_w, s_buf, recv_s, recv_a, a_buf, side_a, side_b, side_p, side_pp, side_c,
    prod, ent, total_buf, recv_t, c_buf, recv_c, e_send, recv_e, cnt_buf, recv_cnt,
    corr, recv_cz, corr_x, recv_cx,
    sem_cnt, rsem_cnt, sem_a, rsem_a, sem_s, rsem_s, sem_e, rsem_e, sem_t, rsem_t, sem_c, rsem_c,
    sem_cz, rsem_cz, sem_cx, rsem_cx,
):
    x, z, c, e = (lax.axis_index(name) for name in ("x", "z", "c", "e"))
    me = z * NC + c

    def zc_peers():
        for dz in Z_OFFSETS:
            for dc in (1, 0):
                if dz == 0 and dc == 0:
                    continue
                pz, pc = lax.rem(z + dz, NZ), lax.rem(c + dc, NC)
                yield pz * NC + pc, {"z": pz, "c": pc}

    def copy(src, dst, ssem, rsem, device):
        return pltpu.make_async_remote_copy(
            src_ref=src, dst_ref=dst, send_sem=ssem, recv_sem=rsem, device_id=device, device_id_type=MESH
        )

    recv_a[...] = jnp.zeros_like(recv_a)
    barrier = pltpu.get_barrier_semaphore()
    for _, device in zc_peers():
        pl.semaphore_signal(barrier, inc=1, device_id=device, device_id_type=MESH)
    for k in range(1, NX):
        pl.semaphore_signal(barrier, inc=1, device_id={"x": lax.rem(x + k, NX)}, device_id_type=MESH)
    for k in range(1, NE):
        pl.semaphore_signal(barrier, inc=1, device_id={"e": lax.rem(e + k, NE)}, device_id_type=MESH)

    contact = contact_ref[...].astype(F32)
    counts = jnp.sum(contact, axis=1, keepdims=True)
    cnt_buf[...] = jnp.zeros_like(cnt_buf)
    cnt_buf[0:4, :] = jnp.broadcast_to(counts, (4, LANES))
    pl.semaphore_wait(barrier, GROUP - 1 + NX - 1 + NE - 1)

    count_copies = []
    for k in range(1, NE):
        cp = copy(cnt_buf, recv_cnt.at[e], sem_cnt.at[k], rsem_cnt.at[e], {"e": lax.rem(e + k, NE)})
        cp.start()
        count_copies.append(cp)

    stiff, damp, grav = par_ref[0:1], par_ref[1:2], par_ref[2:3]
    cstiff, cdamp = par_ref[3:4], par_ref[4:5]
    lane = lax.broadcasted_iota(jnp.int32, (8, LANES), 1)
    row = lax.broadcasted_iota(jnp.int32, (8, LANES), 0)
    flip[...] = jnp.zeros_like(flip)
    flip[0:STATE, :] = init_ref[...]
    init_t[...] = jnp.transpose(flip[...])
    flip[...] = jnp.zeros_like(flip)
    flip[0:4, :] = contact
    contact8 = flip[0:8, :]
    for j in range(2):
        mine = row == jnp.where(lane < HALF, j, 2 + j)
        kk[j] = (stiff + exact_ta(contact8, jnp.where(mine, jnp.broadcast_to(cstiff, (8, LANES)), 0.0))) * TWO_PI
        dd[j] = (damp + exact_ta(contact8, jnp.where(mine, jnp.broadcast_to(cdamp, (8, LANES)), 0.0))) * (TWO_PI / H)
    flip[0:8, :] = jnp.zeros((8, ENV), F32)
    for j in range(2):
        flip[0:DOF, :] = torque_ref[j]
        flip[HALF : HALF + DOF, :] = torque_ref[2 + j]
        tau[j] = jnp.transpose(flip[...])
    hi, lo = split(block_ref[...] * (H * H / TWO_PI))
    nfine[0:LANES, 0:LANES] = hi
    nfine[0:LANES, LANES:] = lo
    nfine[LANES:, 0:LANES] = hi
    nfine[LANES:, LANES:] = lo

    sums = cnt_buf[...]
    for k in range(1, NE):
        p = lax.rem(e + k, NE)
        copy(cnt_buf, recv_cnt.at[p], sem_cnt.at[k], rsem_cnt.at[p], {"e": p}).wait_recv()
        sums = sums + recv_cnt[p]
    mean = sums * (1.0 / (ENV * NE))
    lane1 = lane[0:1]
    springs, frictions = [], []
    for j in range(2):
        m = jnp.where(lane1 < HALF, mean[j : j + 1], mean[2 + j : 3 + j])
        springs.append(stiff + grav + m * cstiff)
        frictions.append(damp + m * cdamp)

    def coarse(q, v, forced):
        for j in range(2):
            force = -(springs[j] * q + frictions[j] * v)
            if forced:
                force = force + tau[j]
            v = v + DT * exact(force, block_ref[...])
            q = q + DT * v
        return q, v

    eye = (
        lax.broadcasted_iota(jnp.int32, (LANES, LANES), 0) == lax.broadcasted_iota(jnp.int32, (LANES, LANES), 1)
    ).astype(F32)
    none = jnp.zeros((LANES, LANES), F32)
    mq, mv = coarse(jnp.concatenate([eye, none], axis=0), jnp.concatenate([none, eye], axis=0), False)
    mf = jnp.concatenate([mq, mv], axis=1)
    put_pair(mf_w, mf)
    map0 = exact_ta(pick_ref[0], exact(mf, pick_ref[0]))
    map1 = exact_ta(pick_ref[1], exact(mf, pick_ref[1]))
    a_buf[...] = exact(map0, map1)
    recv_a[me, 0:ROWS, :] = a_buf[0:ROWS, :]
    a_copies = []
    for p, device in zc_peers():
        cp = copy(
            a_buf.at[pl.ds(0, ROWS)], recv_a.at[me, pl.ds(0, ROWS)], sem_a.at[p], rsem_a.at[me], device
        )
        cp.start()
        a_copies.append(cp)
    put_pair(zf_w, exact(pick_ref[0], map1) + pick_ref[1])
    put_pair(ze_w, exact_tb(eye, pick_ref[0]) + exact_tb(map0, pick_ref[1]))

    fq, fv = coarse(jnp.zeros((ENV, LANES), F32), jnp.zeros((ENV, LANES), F32), True)
    free[:, 0:LANES] = fq
    free[:, LANES:] = fv
    jall[...] = jnp.zeros_like(jall)
    gee[...] = jnp.zeros_like(gee)
    ends[...] = jnp.zeros_like(ends)
    corr[...] = jnp.zeros_like(corr)
    for cp in count_copies:
        cp.wait_send()

    def fine():
        q_ref[...] = start[:, 0:LANES] * (1.0 / TWO_PI)
        v_ref[...] = start[:, LANES:] * (H / TWO_PI)
        coef = [grav * value for value in SINE]

        def horizon(j, unused):
            def substep(counter, unused2):
                for part in range(2):
                    rows = slice(part * (ENV // 2), (part + 1) * (ENV // 2))
                    q, v = q_ref[rows], v_ref[rows]
                    n = (q + MAGIC) - MAGIC
                    r = q - n
                    r2 = r * r
                    poly = coef[-1] * r2 + coef[-2]
                    for value in coef[-3::-1]:
                        poly = poly * r2 + value
                    force = tau[j, rows] - kk[j, rows] * q - dd[j, rows] * v - r * poly
                    hi, lo = split(force)
                    out = dot(jnp.concatenate([hi, lo], axis=1), nfine[...])
                    v = v + (out[:, 0:LANES] + out[:, LANES:])
                    v_ref[rows] = v
                    q_ref[rows] = q + v
                return unused2

            return lax.fori_loop(0, SUB, substep, unused, unroll=4)

        lax.fori_loop(0, 2, horizon, 0)
        free[:, 0:LANES] = q_ref[...] * TWO_PI
        free[:, LANES:] = v_ref[...] * (TWO_PI / H)

    def settle(slot):
        new = gee[...] + jall[...]
        change = new - ends[...]
        ends[...] = new
        square = change * change
        lanes2 = lax.broadcasted_iota(jnp.int32, (8, LANES), 1)
        first = (lanes2 < HALF).astype(F32)
        folded = square[:, 0:LANES] + square[:, LANES:]
        sum0 = exact_tb(first, folded)
        sum1 = exact_tb(1.0 - first, folded)
        corr[pl.ds(slot, 1), :] = jnp.sqrt(jnp.maximum(sum0, sum1))[0:1]

    def products():
        for i in range(4):
            acc = recv_a[4 * i]
            prod[4 * i + 0] = acc
            for j in range(1, 4):
                put_side(side_a, 4 * i + j, recv_a[4 * i + j])
                put_side(side_p, 4 * i + j, acc)
                acc = exact(acc, recv_a[4 * i + j])
                prod[4 * i + j] = acc
            put_side(side_b, i, acc)
        before = prod[3]
        for j in range(1, 4):
            put_side(side_pp, j, prod[j - 1])
        for i in range(1, 4):
            put_side(side_pp, 4 * i, before)
            for j in range(1, 4):
                put_side(side_pp, 4 * i + j, exact(before, prod[4 * i + j - 1]))
            before = exact(before, prod[4 * i + 3])
        c_buf[...] = before
        for k in range(1, NX):

            @pl.when(x + k < NX)
            def _():
                copy(c_buf, recv_c.at[x], sem_c.at[k], rsem_c.at[x], {"x": lax.rem(x + k, NX)}).start()

        for k in range(NX - 1):

            @pl.when(x > k)
            def _():
                copy(c_buf, recv_c.at[k], sem_c.at[k], rsem_c.at[k], {"x": k}).wait_recv()
                put_side(side_c, k, recv_c[k])

    def sweep(k, unused):
        @pl.when(k > 0)
        def _():
            fine()

        fresh = free[...] - gee[...]
        s_buf[...] = wide(fresh, zf_w)
        recv_s[k, me] = s_buf[pl.ds(me * BLOCK, BLOCK), :]
        s_copies = []
        for p, device in zc_peers():
            cp = copy(s_buf.at[pl.ds(p * BLOCK, BLOCK)], recv_s.at[k, me], sem_s.at[p], rsem_s.at[k, me], device)
            cp.start()
            s_copies.append(cp)

        settle(lax.max(k - 2, 0))
        jall[...] = fresh
        low = lax.broadcasted_iota(jnp.int32, (ENV, LANES), 1) < HALF
        for part in range(2):
            cols = slice(part * LANES, (part + 1) * LANES)
            jshift[:, cols] = jnp.where(low, 0.0, pltpu.roll(fresh[:, cols], HALF, 1))

        @pl.when(k == 0)
        def _():
            for p, device in zc_peers():
                copy(
                    a_buf.at[pl.ds(0, ROWS)], recv_a.at[p, pl.ds(0, ROWS)], sem_a.at[p], rsem_a.at[p], device
                ).wait_recv()
            products()

        for p, device in zc_peers():
            copy(s_buf.at[pl.ds(0, BLOCK)], recv_s.at[k, p], sem_s.at[p], rsem_s.at[k, p], device).wait_recv()

        inside = {}
        totals = []
        for i in range(4):
            acc = recv_s[k, 4 * i]
            for j in range(1, 4):
                inside[i, j] = acc
                acc = small(acc, side_a[4 * i + j]) + recv_s[k, 4 * i + j]
            totals.append(acc)
        entry = [None, totals[0]]
        for i in range(1, 4):
            entry.append(small(entry[i], side_b[i]) + totals[i])
        total_buf[...] = entry[4]
        for d in range(1, NX):

            @pl.when(x + d < NX)
            def _():
                copy(total_buf, recv_t.at[k, x], sem_t.at[d], rsem_t.at[k, x], {"x": lax.rem(x + d, NX)}).start()

        for i in range(4):
            if i > 0:
                ent[4 * i] = entry[i]
            for j in range(1, 4):
                value = inside[i, j]
                if i > 0:
                    value = small(entry[i], side_p[4 * i + j]) + value
                ent[4 * i + j] = value
        ent[0] = init_t[pl.ds(me * BLOCK, BLOCK), :]
        for d in range(NX - 1):

            @pl.when(x > d)
            def _():
                copy(total_buf, recv_t.at[k, d], sem_t.at[d], rsem_t.at[k, d], {"x": d}).wait_recv()
                ent[0] = small(ent[0], side_c[d]) + recv_t[k, d]

        first = ent[0]
        e_send[0] = first
        for d in range(1, GROUP):
            e_send[d] = small(first, side_pp[d]) + ent[d]
        recv_e[k, me] = e_send[me]
        e_copies = []
        for p, device in zc_peers():
            cp = copy(e_send.at[p], recv_e.at[k, me], sem_e.at[p], rsem_e.at[k, me], device)
            cp.start()
            e_copies.append(cp)
        for p, device in zc_peers():
            copy(e_send.at[p], recv_e.at[k, p], sem_e.at[p], rsem_e.at[k, p], device).wait_recv()

        arrived = recv_e[k].reshape(ENV, LANES)
        begin = wide(arrived, ze_w) + jshift[...]
        start[...] = begin
        gee[...] = wide(begin, mf_w)
        for cp in s_copies:
            cp.wait_send()
        for cp in e_copies:
            cp.wait_send()
        for d in range(1, NX):

            @pl.when(x + d < NX)
            def _():
                copy(total_buf, recv_t.at[k, x], sem_t.at[d], rsem_t.at[k, x], {"x": lax.rem(x + d, NX)}).wait_send()

        return unused

    lax.fori_loop(0, SWEEPS, sweep, 0)

    settle(ITERS - 1)
    cz_copies = []
    recv_cz[me] = corr[...]
    for p, device in zc_peers():
        cp = copy(corr, recv_cz.at[me], sem_cz.at[p], rsem_cz.at[me], device)
        cp.start()
        cz_copies.append(cp)
    for s in range(2):
        final_ref[s] = lax.dot_general(
            pick_ref[s], ends[...], (((0,), (1,)), ((), ())), precision=HIGHEST, preferred_element_type=F32
        )[0:STATE]
    for p, device in zc_peers():
        copy(corr, recv_cz.at[p], sem_cz.at[p], rsem_cz.at[p], device).wait_recv()
    corr_x[...] = jnp.max(recv_cz[...], axis=0)
    cx_copies = []
    for d in range(1, NX):
        cp = copy(corr_x, recv_cx.at[x], sem_cx.at[d], rsem_cx.at[x], {"x": lax.rem(x + d, NX)})
        cp.start()
        cx_copies.append(cp)
    best = corr_x[...]
    for d in range(1, NX):
        p = lax.rem(x + d, NX)
        copy(corr_x, recv_cx.at[p], sem_cx.at[d], rsem_cx.at[p], {"x": p}).wait_recv()
        best = jnp.maximum(best, recv_cx[p])
    corr_out_ref[...] = best[0:ITERS]
    for cp in a_copies + cz_copies + cx_copies:
        cp.wait_send()
    for k in range(1, NX):

        @pl.when(x + k < NX)
        def _():
            copy(c_buf, recv_c.at[x], sem_c.at[k], rsem_c.at[x], {"x": lax.rem(x + k, NX)}).wait_send()


def scratch():
    def v(*shape, dtype=F32):
        return pltpu.VMEM(shape, dtype)

    dma = pltpu.SemaphoreType.DMA
    return [
        v(LANES, ENV),
        v(2, ENV, LANES),
        v(2, ENV, LANES),
        v(2, ENV, LANES),
        v(ENV, LANES),
        v(ENV, LANES),
        v(ENV, LANES),
        v(2 * LANES, 2 * LANES, dtype=BF16),
        v(ENV, 2 * LANES),
        v(ENV, 2 * LANES),
        v(ENV, 2 * LANES),
        v(ENV, 2 * LANES),
        v(ENV, 2 * LANES),
        v(ENV, 2 * LANES),
        v(2, 2 * LANES, 2 * LANES, dtype=BF16),
        v(2, 2 * LANES, LANES, dtype=BF16),
        v(2, LANES, 2 * LANES, dtype=BF16),
        v(ENV, LANES),
        v(SWEEPS, GROUP, BLOCK, LANES),
        v(GROUP, LANES, LANES),
        v(LANES, LANES),
        v(GROUP, LANES, 2 * LANES, dtype=BF16),
        v(4, LANES, 2 * LANES, dtype=BF16),
        v(GROUP, LANES, 2 * LANES, dtype=BF16),
        v(GROUP, LANES, 2 * LANES, dtype=BF16),
        v(NX, LANES, 2 * LANES, dtype=BF16),
        v(GROUP, LANES, LANES),
        v(GROUP, BLOCK, LANES),
        v(BLOCK, LANES),
        v(SWEEPS, NX, BLOCK, LANES),
        v(LANES, LANES),
        v(NX, LANES, LANES),
        v(GROUP, BLOCK, LANES),
        v(SWEEPS, GROUP, BLOCK, LANES),
        v(8, LANES),
        v(NE, 8, LANES),
        v(8, ENV),
        v(GROUP, 8, ENV),
        v(8, ENV),
        v(NX, 8, ENV),
        dma((NE,)), dma((NE,)),
        dma((GROUP,)), dma((GROUP,)),
        dma((GROUP,)), dma((SWEEPS, GROUP)),
        dma((GROUP,)), dma((SWEEPS, GROUP)),
        dma((NX,)), dma((SWEEPS, NX)),
        dma((NX,)), dma((NX,)),
        dma((GROUP,)), dma((GROUP,)),
        dma((NX,)), dma((NX,)),
    ]


def shards(
    init_state, torque, contact, mass_inverse, stiffness, damping, gravity, contact_stiffness, contact_damping
):
    params = jnp.stack([stiffness, damping, gravity, contact_stiffness, contact_damping])
    params = jnp.pad(params, ((0, 3), (0, HALF - DOF)))
    params = jnp.concatenate([params, params], axis=1)
    blocks = jnp.pad(mass_inverse, ((0, 0), (0, HALF - DOF), (0, HALF - DOF)))
    zero = jnp.zeros((HALF, HALF), F32)
    block = jnp.concatenate(
        [jnp.concatenate([blocks[0], zero], axis=1), jnp.concatenate([zero, blocks[1]], axis=1)], axis=0
    )
    vmem = pl.BlockSpec(memory_space=pltpu.VMEM)
    return pl.pallas_call(
        body,
        out_shape=(
            jax.ShapeDtypeStruct((2, STATE, ENV), F32),
            jax.ShapeDtypeStruct((ITERS, ENV), F32),
        ),
        in_specs=[vmem] * 6,
        out_specs=(vmem, vmem),
        scratch_shapes=scratch(),
        compiler_params=pltpu.CompilerParams(collective_id=0, has_side_effects=True, vmem_limit_bytes=48 * 2**20),
        name="parareal",
    )(init_state, torque, contact, block, params, jnp.asarray(PICK))


def solution(mesh):
    torus = Mesh(mesh.devices.reshape(NX, NZ, NC, NE), ("x", "z", "c", "e"))
    return jax.shard_map(
        shards,
        mesh=torus,
        in_specs=(
            P(None, "e"),
            P(TM, None, "e"),
            P(TM, "e"),
            P(TM, None, None),
            P(),
            P(),
            P(),
            P(),
            P(),
        ),
        out_specs=(P(TM, None, "e"), P(None, "e")),
        check_vma=False,
    )
```

time: 368 us -> 138 us (0.38); the launches traced: 363 us -> 138 us
  blocking collectives: 196 us -> 0 us
  Pallas kernels: 0 us -> 134 us
  matrix products: 122 us -> 0 us
  starting transfers between devices: 21.7 us -> 0 us
  waiting for transfers between devices: 12.8 us -> 0 us
    all_gather x15 -> x0, blocking collectives: 196 us -> none  [prefix_by_axis(): pieces = jax.tree.map(lambda part: lax.all_gather(part, axis), running)]
    pallas_call x0 -> x1, Pallas kernels: none -> 134 us  [shards(): pl.pallas_call(body, out_shape=(jax.ShapeDtypeStruct((2, STATE, ENV), F32...]
    dot_general x291 -> x0, matrix products: 122 us -> none  [the longest x288 121 us: exact_dot(): jnp.dot(left, right, precision=lax.Precision.HIGHEST, preferred_element_t...]
    all_to_all x2 -> x0, starting transfers between devices: 21.7 us -> none  [sent_to_all(): return lax.all_to_all(copies, axis, split_axis=0, concat_axis=0, tiled=True)]
    all_to_all x2 -> x0, waiting for transfers between devices: 12.8 us -> none  [sent_to_all(): return lax.all_to_all(copies, axis, split_axis=0, concat_axis=0, tiled=True)]
  transfers between devices with their start and end apart: 2 -> 0, of which waited for: 2 -> 0; matrix products, arithmetic and copies ran while one was open for 0% -> 0% of each run, Pallas kernels for 0% -> 0%
where the time goes in v1:
time: 138 us
  Pallas kernels  134 us (97%)
  local copies, waits for them, and re-layouts  3.78 us (3%)
    pallas_call x1, Pallas kernels, shards(): pl.pallas_call(body, out_shape=(jax.ShapeDtypeStruct((2, STATE, ENV), F32...  134 us
    unnamed x21, local copies, waits for them, and re-layouts  3.01 us

profile of v1, /device:TPU:1, one launch (start us, length us, event | category | flops | bytes accessed | tf_op | source)
XLA Modules:
  0.0 138.1 jit_solution(15401622474846638836)
XLA Ops:
  0.6 0.0 copy-start.7
  0.6 0.0 copy-start.8
  0.7 0.0 copy-start.4
  0.7 0.0 copy-start.5
  0.7 0.0 copy-start.6
  0.7 0.6 copy-done.7
  1.3 0.0 copy-done.8
  1.3 0.0 copy-done.4
  1.3 0.0 copy-done.5
  1.3 0.0 copy-done.6
  1.4 0.1 pad_maximum_fusion.par_ref
  1.5 0.0 copy-start.3
  1.5 0.8 copy.12
  2.3 0.0 copy-start
  2.3 0.1 select_maximum_fusion.block_ref
  2.4 0.0 copy-done.3
  2.4 0.0 copy-start.1
  2.4 0.0 copy-start.2
  2.4 0.8 copy-done
  3.2 0.1 copy-done.1
  3.3 0.0 copy-done.2
  3.3 133.5 %parareal.1 = (f32[2,70,256]{2,1,0:T(8,128)S(1)}, f32[3,256]{1,0:T(4,128)S(1)}) custom-call(f32[70,256]{1,0:T(8,128)S(1)} %copy-done.1, f32[4,35,256]{2,1,0:T(8,128)S(1)} %copy.13.torque_ref, s32[4,256]{1,0:T(4,128)S(1)} %copy-done.2, f32[128,128]{1,0:T(8,128)S(1)} %select_maximum_fusion.block_ref, f32[8,128]{1,0:T(8,128)S(1)} %pad_maximum_fusion.par_ref, ...), custom_call_target="tpu_custom_call" | custom-call | tf_op jit(solution)/shard_map/parareal/pallas_call | solution.py:509
  136.8 0.7 copy.14
  137.5 0.6 copy.16
  (4 shorter events, 0.1 us)
Async XLA Ops:
  0.6 0.7 copy-start.7
  0.6 0.7 copy-start.8
  0.7 0.7 copy-start.4
  0.7 0.7 copy-start.5
  0.7 0.7 copy-start.6
  1.5 0.9 copy-start.3
  2.3 1.0 copy-start
  2.4 0.9 copy-start.1
  2.4 0.9 copy-start.2

commit v2 on v1

--- a/solution.py
+++ b/solution.py
@@ -20,7 +20,8 @@
 BLOCK = ENV // GROUP
 LANES = 128
 HALF = 64
-ROWS = 72
+MROWS = 80
+NROWS = 40
 DT = 0.05
 H = DT / SUB
 TWO_PI = 2.0 * math.pi
@@ -67,6 +68,13 @@
     return hi, lo
 
 
+def split3(x):
+    hi = x.astype(BF16)
+    rest = x - hi.astype(F32)
+    mid = rest.astype(BF16)
+    return hi, mid, (rest - mid.astype(F32)).astype(BF16)
+
+
 def dot(a, b):
     return jnp.dot(a, b, preferred_element_type=F32)
 
@@ -86,6 +94,16 @@
 def wide(x, weights):
     hi, lo = split(x)
     return dot(hi, weights[0]) + dot(lo, weights[0]) + dot(hi, weights[1])
+
+
+def pick_right(x, pick):
+    hi, mid, lo = split3(x)
+    return dot(hi, pick) + dot(mid, pick) + dot(lo, pick)
+
+
+def pick_left(pick, x):
+    hi, mid, lo = split3(x)
+    return dot(pick, hi) + dot(pick, mid) + dot(pick, lo)
 
 
 def put_pair(ref, value):
@@ -96,25 +114,27 @@
 
 def put_side(ref, index, value):
     hi, lo = split(value)
-    ref[index, :, 0:LANES] = hi
-    ref[index, :, LANES:] = lo
+    ref[index, 0:MROWS, 0:LANES] = hi
+    ref[index, 0:MROWS, LANES:] = lo
 
 
 def small(x, weights):
+    rows = x.shape[0]
     hi, lo = split(x)
     out = dot(jnp.concatenate([hi, lo], axis=0), weights)
     both = out[:, 0:LANES] + out[:, LANES:]
-    return both[0:BLOCK] + both[BLOCK:]
+    return both[0:rows] + both[rows:]
 
 
 def body(
-    init_ref, torque_ref, contact_ref, block_ref, par_ref, pick_ref,
+    init_in, torque_in, contact_in, minv_in, stiff_in, damp_in, grav_in, cstiff_in, cdamp_in, pick_in, turn_in,
     final_ref, corr_out_ref,
-    flip, tau, kk, dd, q_ref, v_ref, init_t, nfine, free, jall, start, gee, ends, jshift,
-    mf_w, zf_w, ze_w, s_buf, recv_s, recv_a, a_buf, side_a, side_b, side_p, side_pp, side_c,
+    init_ref, torque_ref, contact_ref, minv_ref, stiff_ref, damp_ref, grav_ref, cstiff_ref, cdamp_ref, pick_ref, turn_ref,
+    in_sem, par_ref, block_ref, flip, tau, kk, dd, q_ref, v_ref, init_t, nfine, free, jall, start, gee, ends, jshift,
+    mf_w, zf_w, ze_w, s_buf, recv_s, n_buf, recv_n, m_buf, recv_m, side_n, side_a, side_b, side_p, side_pp, side_c,
     prod, ent, total_buf, recv_t, c_buf, recv_c, e_send, recv_e, cnt_buf, recv_cnt,
     corr, recv_cz, corr_x, recv_cx,
-    sem_cnt, rsem_cnt, sem_a, rsem_a, sem_s, rsem_s, sem_e, rsem_e, sem_t, rsem_t, sem_c, rsem_c,
+    sem_cnt, rsem_cnt, sem_n, rsem_n, sem_m, rsem_m, sem_s, rsem_s, sem_e, rsem_e, sem_t, rsem_t, sem_c, rsem_c,
     sem_cz, rsem_cz, sem_cx, rsem_cx,
 ):
     x, z, c, e = (lax.axis_index(name) for name in ("x", "z", "c", "e"))
@@ -133,7 +153,16 @@
             src_ref=src, dst_ref=dst, send_sem=ssem, recv_sem=rsem, device_id=device, device_id_type=MESH
         )
 
-    recv_a[...] = jnp.zeros_like(recv_a)
+    sources = (
+        contact_in, minv_in, stiff_in, damp_in, grav_in, cstiff_in, cdamp_in, init_in, torque_in, pick_in, turn_in,
+    )
+    targets = (
+        contact_ref, minv_ref, stiff_ref, damp_ref, grav_ref, cstiff_ref, cdamp_ref,
+        init_ref, torque_ref, pick_ref, turn_ref,
+    )
+    loads = [pltpu.make_async_copy(a, b, in_sem.at[i]) for i, (a, b) in enumerate(zip(sources, targets))]
+    for load in loads:
+        load.start()
     barrier = pltpu.get_barrier_semaphore()
     for _, device in zc_peers():
         pl.semaphore_signal(barrier, inc=1, device_id=device, device_id_type=MESH)
@@ -142,10 +171,36 @@
     for k in range(1, NE):
         pl.semaphore_signal(barrier, inc=1, device_id={"e": lax.rem(e + k, NE)}, device_id_type=MESH)
 
+    for side in (side_a, side_b, side_p, side_pp, side_c, side_n):
+        side[...] = jnp.zeros_like(side)
+    for load in loads:
+        load.wait()
     contact = contact_ref[...].astype(F32)
     counts = jnp.sum(contact, axis=1, keepdims=True)
     cnt_buf[...] = jnp.zeros_like(cnt_buf)
     cnt_buf[0:4, :] = jnp.broadcast_to(counts, (4, LANES))
+    lane = lax.broadcasted_iota(jnp.int32, (8, LANES), 1)
+    row = lax.broadcasted_iota(jnp.int32, (8, LANES), 0)
+    par_ref[...] = jnp.zeros_like(par_ref)
+    for i, ref in enumerate((stiff_ref, damp_ref, grav_ref, cstiff_ref, cdamp_ref)):
+        par_ref[i : i + 1, 0:DOF] = ref[...]
+    par_one = par_ref[...]
+    par_ref[...] = par_one + pltpu.roll(par_one, HALF, 1)
+    flip[...] = jnp.zeros_like(flip)
+    flip[0:DOF, 0:DOF] = minv_ref[:, 1, :]
+    shifted = pltpu.roll(flip[0:NROWS, 0:LANES], HALF, 1)
+    flip[0:DOF, 0:DOF] = minv_ref[:, 0, :]
+    packed = flip[0:NROWS, 0:LANES] + shifted
+    n_buf[...] = packed
+    recv_n[me] = packed
+    low40 = lax.broadcasted_iota(jnp.int32, (NROWS, LANES), 1) < HALF
+    def clear(i, unused):
+        block_ref[pl.ds(pl.multiple_of(i * HALF, HALF), HALF), :] = jnp.zeros((HALF, LANES), F32)
+        return unused
+
+    lax.fori_loop(0, 2, clear, 0)
+    block_ref[0:NROWS, :] = jnp.where(low40, packed, 0.0)
+    block_ref[HALF : HALF + NROWS, :] = jnp.where(low40, 0.0, packed)
     pl.semaphore_wait(barrier, GROUP - 1 + NX - 1 + NE - 1)
 
     count_copies = []
@@ -153,12 +208,14 @@
         cp = copy(cnt_buf, recv_cnt.at[e], sem_cnt.at[k], rsem_cnt.at[e], {"e": lax.rem(e + k, NE)})
         cp.start()
         count_copies.append(cp)
+    n_copies = []
+    for p, device in zc_peers():
+        cp = copy(n_buf, recv_n.at[me], sem_n.at[p], rsem_n.at[me], device)
+        cp.start()
+        n_copies.append(cp)
 
     stiff, damp, grav = par_ref[0:1], par_ref[1:2], par_ref[2:3]
     cstiff, cdamp = par_ref[3:4], par_ref[4:5]
-    lane = lax.broadcasted_iota(jnp.int32, (8, LANES), 1)
-    row = lax.broadcasted_iota(jnp.int32, (8, LANES), 0)
-    flip[...] = jnp.zeros_like(flip)
     flip[0:STATE, :] = init_ref[...]
     init_t[...] = jnp.transpose(flip[...])
     flip[...] = jnp.zeros_like(flip)
@@ -170,8 +227,8 @@
         dd[j] = (damp + exact_ta(contact8, jnp.where(mine, jnp.broadcast_to(cdamp, (8, LANES)), 0.0))) * (TWO_PI / H)
     flip[0:8, :] = jnp.zeros((8, ENV), F32)
     for j in range(2):
-        flip[0:DOF, :] = torque_ref[j]
-        flip[HALF : HALF + DOF, :] = torque_ref[2 + j]
+        flip[0:DOF, :] = torque_ref[:, j, :]
+        flip[HALF : HALF + DOF, :] = torque_ref[:, 2 + j, :]
         tau[j] = jnp.transpose(flip[...])
     hi, lo = split(block_ref[...] * (H * H / TWO_PI))
     nfine[0:LANES, 0:LANES] = hi
@@ -185,6 +242,13 @@
         copy(cnt_buf, recv_cnt.at[p], sem_cnt.at[k], rsem_cnt.at[p], {"e": p}).wait_recv()
         sums = sums + recv_cnt[p]
     mean = sums * (1.0 / (ENV * NE))
+    m_buf[...] = mean
+    recv_m[me] = mean
+    m_copies = []
+    for p, device in zc_peers():
+        cp = copy(m_buf, recv_m.at[me], sem_m.at[p], rsem_m.at[me], device)
+        cp.start()
+        m_copies.append(cp)
     lane1 = lane[0:1]
     springs, frictions = [], []
     for j in range(2):
@@ -208,19 +272,10 @@
     mq, mv = coarse(jnp.concatenate([eye, none], axis=0), jnp.concatenate([none, eye], axis=0), False)
     mf = jnp.concatenate([mq, mv], axis=1)
     put_pair(mf_w, mf)
-    map0 = exact_ta(pick_ref[0], exact(mf, pick_ref[0]))
-    map1 = exact_ta(pick_ref[1], exact(mf, pick_ref[1]))
-    a_buf[...] = exact(map0, map1)
-    recv_a[me, 0:ROWS, :] = a_buf[0:ROWS, :]
-    a_copies = []
-    for p, device in zc_peers():
-        cp = copy(
-            a_buf.at[pl.ds(0, ROWS)], recv_a.at[me, pl.ds(0, ROWS)], sem_a.at[p], rsem_a.at[me], device
-        )
-        cp.start()
-        a_copies.append(cp)
-    put_pair(zf_w, exact(pick_ref[0], map1) + pick_ref[1])
-    put_pair(ze_w, exact_tb(eye, pick_ref[0]) + exact_tb(map0, pick_ref[1]))
+    map0 = pick_left(turn_ref[0], pick_right(mf, pick_ref[0]))
+    map1 = pick_left(turn_ref[1], pick_right(mf, pick_ref[1]))
+    put_pair(zf_w, pick_left(pick_ref[0], map1) + pick_ref[1].astype(F32))
+    put_pair(ze_w, turn_ref[0].astype(F32) + pick_right(map0, turn_ref[1]))
 
     fq, fv = coarse(jnp.zeros((ENV, LANES), F32), jnp.zeros((ENV, LANES), F32), True)
     free[:, 0:LANES] = fq
@@ -272,39 +327,61 @@
         folded = square[:, 0:LANES] + square[:, LANES:]
         sum0 = exact_tb(first, folded)
         sum1 = exact_tb(1.0 - first, folded)
-        corr[pl.ds(slot, 1), :] = jnp.sqrt(jnp.maximum(sum0, sum1))[0:1]
+        largest = jnp.sqrt(jnp.maximum(sum0, sum1))[0:1]
+        corr[pl.ds(slot, 1), :] = largest[:, 0:LANES]
+        corr[pl.ds(slot + 4, 1), :] = largest[:, LANES:]
+
+    def maps(part, unused):
+        rr = lax.broadcasted_iota(jnp.int32, (MROWS, LANES), 0)
+        ll = lax.broadcasted_iota(jnp.int32, (MROWS, LANES), 1)
+        base_q = ((rr == ll) & (ll < DOF)).astype(F32)
+        base_v = ((rr == ll + DOF) & (ll < DOF)).astype(F32)
+        keep = lane[0:1] < HALF
+        one = [jnp.where(keep, par_ref[i : i + 1], 0.0) for i in range(5)]
+        for u in range(8):
+            p = part * 8 + u
+            n_both = recv_n[p]
+            means = recv_m[p]
+            q, v = base_q, base_v
+            for s in range(2):
+                n_one = jnp.where(low40, pltpu.roll(n_both, HALF, 1) if s else n_both, 0.0)
+                hi, lo = split(n_one)
+                side_n[2 * u + s, 0:NROWS, 0:LANES] = hi
+                side_n[2 * u + s, 0:NROWS, LANES:] = lo
+                for j in range(2):
+                    m = means[2 * s + j : 2 * s + j + 1]
+                    spring = one[0] + one[2] + m * one[3]
+                    friction = one[1] + m * one[4]
+                    v = v - DT * small(spring * q + friction * v, side_n[2 * u + s])
+                    q = q + DT * v
+            full = q + pltpu.roll(v, DOF, 1)
+            prod[p] = full
+            put_side(side_a, p, full)
+        return unused
 
     def products():
+        lax.fori_loop(0, 2, maps, 0)
         for i in range(4):
-            acc = recv_a[4 * i]
-            prod[4 * i + 0] = acc
+            acc = prod[4 * i]
             for j in range(1, 4):
-                put_side(side_a, 4 * i + j, recv_a[4 * i + j])
                 put_side(side_p, 4 * i + j, acc)
-                acc = exact(acc, recv_a[4 * i + j])
-                prod[4 * i + j] = acc
+                acc = small(acc, side_a[4 * i + j])
             put_side(side_b, i, acc)
-        before = prod[3]
+            if i == 0:
+                before = acc
         for j in range(1, 4):
-            put_side(side_pp, j, prod[j - 1])
+            side_pp[j] = side_p[j]
         for i in range(1, 4):
             put_side(side_pp, 4 * i, before)
             for j in range(1, 4):
-                put_side(side_pp, 4 * i + j, exact(before, prod[4 * i + j - 1]))
-            before = exact(before, prod[4 * i + 3])
+                put_side(side_pp, 4 * i + j, small(before, side_p[4 * i + j]))
+            before = small(before, side_b[i])
         c_buf[...] = before
         for k in range(1, NX):
 
             @pl.when(x + k < NX)
             def _():
                 copy(c_buf, recv_c.at[x], sem_c.at[k], rsem_c.at[x], {"x": lax.rem(x + k, NX)}).start()
-
-        for k in range(NX - 1):
-
-            @pl.when(x > k)
-            def _():
-                copy(c_buf, recv_c.at[k], sem_c.at[k], rsem_c.at[k], {"x": k}).wait_recv()
-                put_side(side_c, k, recv_c[k])
 
     def sweep(k, unused):
         @pl.when(k > 0)
@@ -330,9 +407,9 @@
         @pl.when(k == 0)
         def _():
             for p, device in zc_peers():
-                copy(
-                    a_buf.at[pl.ds(0, ROWS)], recv_a.at[p, pl.ds(0, ROWS)], sem_a.at[p], rsem_a.at[p], device
-                ).wait_recv()
+                copy(n_buf, recv_n.at[p], sem_n.at[p], rsem_n.at[p], device).wait_recv()
+            for p, device in zc_peers():
+                copy(m_buf, recv_m.at[p], sem_m.at[p], rsem_m.at[p], device).wait_recv()
             products()
 
         for p, device in zc_peers():
@@ -369,6 +446,11 @@
 
             @pl.when(x > d)
             def _():
+                @pl.when(k == 0)
+                def _():
+                    copy(c_buf, recv_c.at[d], sem_c.at[d], rsem_c.at[d], {"x": d}).wait_recv()
+                    put_side(side_c, d, recv_c[d])
+
                 copy(total_buf, recv_t.at[k, d], sem_t.at[d], rsem_t.at[k, d], {"x": d}).wait_recv()
                 ent[0] = small(ent[0], side_c[d]) + recv_t[k, d]
 
@@ -411,8 +493,8 @@
         cp.start()
         cz_copies.append(cp)
     for s in range(2):
-        final_ref[s] = lax.dot_general(
-            pick_ref[s], ends[...], (((0,), (1,)), ((), ())), precision=HIGHEST, preferred_element_type=F32
+        final_ref[:, s, :] = lax.dot_general(
+            pick_ref[s].astype(F32), ends[...], (((0,), (1,)), ((), ())), precision=HIGHEST, preferred_element_type=F32
         )[0:STATE]
     for p, device in zc_peers():
         copy(corr, recv_cz.at[p], sem_cz.at[p], rsem_cz.at[p], device).wait_recv()
@@ -427,8 +509,9 @@
         p = lax.rem(x + d, NX)
         copy(corr_x, recv_cx.at[p], sem_cx.at[d], rsem_cx.at[p], {"x": p}).wait_recv()
         best = jnp.maximum(best, recv_cx[p])
-    corr_out_ref[...] = best[0:ITERS]
-    for cp in a_copies + cz_copies + cx_copies:
+    corr_out_ref[:, 0:LANES] = best[0:ITERS]
+    corr_out_ref[:, LANES:] = best[4 : 4 + ITERS]
+    for cp in n_copies + m_copies + cz_copies + cx_copies:
         cp.wait_send()
     for k in range(1, NX):
 
@@ -443,6 +526,16 @@
 
     dma = pltpu.SemaphoreType.DMA
     return [
+        v(STATE, ENV),
+        v(DOF, 4, ENV),
+        pltpu.VMEM((4, ENV), jnp.int32),
+        v(DOF, 2, DOF),
+        *[v(1, DOF) for _ in range(5)],
+        v(2, 2 * LANES, LANES, dtype=BF16),
+        v(2, LANES, 2 * LANES, dtype=BF16),
+        dma((11,)),
+        v(8, LANES),
+        v(LANES, LANES),
         v(LANES, ENV),
         v(2, ENV, LANES),
         v(2, ENV, LANES),
@@ -462,28 +555,32 @@
         v(2, LANES, 2 * LANES, dtype=BF16),
         v(ENV, LANES),
         v(SWEEPS, GROUP, BLOCK, LANES),
-        v(GROUP, LANES, LANES),
-        v(LANES, LANES),
+        v(NROWS, LANES),
+        v(GROUP, NROWS, LANES),
+        v(8, LANES),
+        v(GROUP, 8, LANES),
+        v(GROUP, LANES, 2 * LANES, dtype=BF16),
         v(GROUP, LANES, 2 * LANES, dtype=BF16),
         v(4, LANES, 2 * LANES, dtype=BF16),
         v(GROUP, LANES, 2 * LANES, dtype=BF16),
         v(GROUP, LANES, 2 * LANES, dtype=BF16),
         v(NX, LANES, 2 * LANES, dtype=BF16),
-        v(GROUP, LANES, LANES),
+        v(GROUP, MROWS, LANES),
         v(GROUP, BLOCK, LANES),
         v(BLOCK, LANES),
         v(SWEEPS, NX, BLOCK, LANES),
-        v(LANES, LANES),
-        v(NX, LANES, LANES),
+        v(MROWS, LANES),
+        v(NX, MROWS, LANES),
         v(GROUP, BLOCK, LANES),
         v(SWEEPS, GROUP, BLOCK, LANES),
         v(8, LANES),
         v(NE, 8, LANES),
-        v(8, ENV),
-        v(GROUP, 8, ENV),
-        v(8, ENV),
-        v(NX, 8, ENV),
+        v(8, LANES),
+        v(GROUP, 8, LANES),
+        v(8, LANES),
+        v(NX, 8, LANES),
         dma((NE,)), dma((NE,)),
+        dma((GROUP,)), dma((GROUP,)),
         dma((GROUP,)), dma((GROUP,)),
         dma((GROUP,)), dma((SWEEPS, GROUP)),
         dma((GROUP,)), dma((SWEEPS, GROUP)),
@@ -497,27 +594,21 @@
 def shards(
     init_state, torque, contact, mass_inverse, stiffness, damping, gravity, contact_stiffness, contact_damping
 ):
-    params = jnp.stack([stiffness, damping, gravity, contact_stiffness, contact_damping])
-    params = jnp.pad(params, ((0, 3), (0, HALF - DOF)))
-    params = jnp.concatenate([params, params], axis=1)
-    blocks = jnp.pad(mass_inverse, ((0, 0), (0, HALF - DOF), (0, HALF - DOF)))
-    zero = jnp.zeros((HALF, HALF), F32)
-    block = jnp.concatenate(
-        [jnp.concatenate([blocks[0], zero], axis=1), jnp.concatenate([zero, blocks[1]], axis=1)], axis=0
-    )
+    params = [p.reshape(1, DOF) for p in (stiffness, damping, gravity, contact_stiffness, contact_damping)]
     vmem = pl.BlockSpec(memory_space=pltpu.VMEM)
-    return pl.pallas_call(
+    final, corrections = pl.pallas_call(
         body,
         out_shape=(
-            jax.ShapeDtypeStruct((2, STATE, ENV), F32),
+            jax.ShapeDtypeStruct((STATE, 2, ENV), F32),
             jax.ShapeDtypeStruct((ITERS, ENV), F32),
         ),
-        in_specs=[vmem] * 6,
+        in_specs=[pl.BlockSpec(memory_space=pltpu.HBM)] * 11,
         out_specs=(vmem, vmem),
         scratch_shapes=scratch(),
-        compiler_params=pltpu.CompilerParams(collective_id=0, has_side_effects=True, vmem_limit_bytes=48 * 2**20),
+        compiler_params=pltpu.CompilerParams(collective_id=0, has_side_effects=True, vmem_limit_bytes=67043328),
         name="parareal",
-    )(init_state, torque, contact, block, params, jnp.asarray(PICK))
+    )(init_state, jnp.swapaxes(torque, 0, 1), contact, jnp.swapaxes(mass_inverse, 0, 1), *params, jnp.asarray(PICK, BF16), jnp.asarray(PICK.transpose(0, 2, 1), BF16))
+    return jnp.swapaxes(final, 0, 1), corrections
 
 
 def solution(mesh):

time: 138 us -> 130 us (0.942)
  Pallas kernels: 134 us -> 127 us
  local copies, waits for them, and re-layouts: 3.78 us -> 2.17 us
    pallas_call x1, Pallas kernels: 134 us -> 127 us  [shards(): pl.pallas_call(body, out_shape=(jax.ShapeDtypeStruct((STATE, 2, ENV), F32...]
    unnamed x21 -> x4, local copies, waits for them, and re-layouts: 3.01 us -> 2.17 us
where the time goes in v2:
time: 130 us
  Pallas kernels  127 us (98%)
  local copies, waits for them, and re-layouts  2.17 us (2%)
    pallas_call x1, Pallas kernels, shards(): pl.pallas_call(body, out_shape=(jax.ShapeDtypeStruct((STATE, 2, ENV), F32...  127 us

profile of v2, /device:TPU:1, one launch (start us, length us, event | category | flops | bytes accessed | tf_op | source)
XLA Modules:
  0.0 130.1 jit_solution(12430273895958405689)
XLA Ops:
  0.6 127.3 %parareal.1 = (f32[70,2,256]{2,1,0:T(2,128)}, f32[3,256]{1,0:T(4,128)}) custom-call(f32[70,256]{1,0:T(8,128)} %init_in.1, f32[35,4,256]{2,1,0:T(4,128)} %bitcast.8, s32[4,256]{1,0:T(4,128)} %contact_in.1, f32[35,2,35]{2,1,0:T(2,128)} %bitcast.10, f32[1,35]{1,0:T(1,128)} %bitcast.11, f32[1,35]{1,0:T(1,128)} %bitcast.12, f32[1,35]{1,0:T(1,128)} %bitcast.13, ...), custom_call_target="tpu_custom_call" | custom-call | tf_op jit(solution)/shard_map/parareal/pallas_call | solution.py:599
  127.9 0.0 copy-start
  127.9 1.6 %copy.15 = f32[2,70,256]{2,0,1:T(2,128)} copy(f32[2,70,256]{2,0,1:T(2,128)} %bitcast.9) | data formatting | bytes 286720
  129.5 0.0 copy-done
  129.5 0.6 copy.16
Async XLA Ops:
  127.9 1.6 %copy-start = (f32[3,256]{1,0:T(4,128)S(1)}, f32[3,256]{1,0:T(4,128)}, u32[]{:S(2)}) copy-start(f32[3,256]{1,0:T(4,128)} %get-tuple-element.9) | copy-start | bytes 9220

commit v3 on v2

--- a/solution.py
+++ b/solution.py
@@ -25,13 +25,14 @@
 DT = 0.05
 H = DT / SUB
 TWO_PI = 2.0 * math.pi
-MAGIC = 12582912.0
 F32 = jnp.float32
 BF16 = jnp.bfloat16
 MESH = pl.DeviceIdType.MESH
 HIGHEST = lax.Precision.HIGHEST
 TM = ("x", "z", "c")
 Z_OFFSETS = (4, 3, 5, 2, 6, 1, 7, 0)
+NEAR_FIRST = ((0, 1, 7, 2), (6, 3, 5, 4))
+NEAR_CHIPS = (1, 7, 2, 6, 3, 5, 4)
 
 
 def sine_coefficients(terms):
@@ -134,7 +135,7 @@
     mf_w, zf_w, ze_w, s_buf, recv_s, n_buf, recv_n, m_buf, recv_m, side_n, side_a, side_b, side_p, side_pp, side_c,
     prod, ent, total_buf, recv_t, c_buf, recv_c, e_send, recv_e, cnt_buf, recv_cnt,
     corr, recv_cz, corr_x, recv_cx,
-    sem_cnt, rsem_cnt, sem_n, rsem_n, sem_m, rsem_m, sem_s, rsem_s, sem_e, rsem_e, sem_t, rsem_t, sem_c, rsem_c,
+    sem_cnt, rsem_cnt, sem_n, rsem_n, sem_m, rsem_m, sem_p, rsem_p, sem_s, rsem_s, sem_e, rsem_e, sem_t, rsem_t, sem_c, rsem_c,
     sem_cz, rsem_cz, sem_cx, rsem_cx,
 ):
     x, z, c, e = (lax.axis_index(name) for name in ("x", "z", "c", "e"))
@@ -147,6 +148,11 @@
                     continue
                 pz, pc = lax.rem(z + dz, NZ), lax.rem(c + dc, NC)
                 yield pz * NC + pc, {"z": pz, "c": pc}
+
+    def chips(offsets):
+        for dz in offsets:
+            pz = lax.rem(z + dz, NZ)
+            yield pz, {"z": pz}
 
     def copy(src, dst, ssem, rsem, device):
         return pltpu.make_async_remote_copy(
@@ -192,7 +198,7 @@
     flip[0:DOF, 0:DOF] = minv_ref[:, 0, :]
     packed = flip[0:NROWS, 0:LANES] + shifted
     n_buf[...] = packed
-    recv_n[me] = packed
+    recv_n[z] = packed
     low40 = lax.broadcasted_iota(jnp.int32, (NROWS, LANES), 1) < HALF
     def clear(i, unused):
         block_ref[pl.ds(pl.multiple_of(i * HALF, HALF), HALF), :] = jnp.zeros((HALF, LANES), F32)
@@ -209,8 +215,8 @@
         cp.start()
         count_copies.append(cp)
     n_copies = []
-    for p, device in zc_peers():
-        cp = copy(n_buf, recv_n.at[me], sem_n.at[p], rsem_n.at[me], device)
+    for p, device in chips(NEAR_CHIPS):
+        cp = copy(n_buf, recv_n.at[z], sem_n.at[p], rsem_n.at[z], device)
         cp.start()
         n_copies.append(cp)
 
@@ -243,10 +249,10 @@
         sums = sums + recv_cnt[p]
     mean = sums * (1.0 / (ENV * NE))
     m_buf[...] = mean
-    recv_m[me] = mean
+    recv_m[z] = mean
     m_copies = []
-    for p, device in zc_peers():
-        cp = copy(m_buf, recv_m.at[me], sem_m.at[p], rsem_m.at[me], device)
+    for p, device in chips(NEAR_CHIPS):
+        cp = copy(m_buf, recv_m.at[z], sem_m.at[p], rsem_m.at[z], device)
         cp.start()
         m_copies.append(cp)
     lane1 = lane[0:1]
@@ -274,8 +280,16 @@
     put_pair(mf_w, mf)
     map0 = pick_left(turn_ref[0], pick_right(mf, pick_ref[0]))
     map1 = pick_left(turn_ref[1], pick_right(mf, pick_ref[1]))
-    put_pair(zf_w, pick_left(pick_ref[0], map1) + pick_ref[1].astype(F32))
-    put_pair(ze_w, turn_ref[0].astype(F32) + pick_right(map0, turn_ref[1]))
+    hi, lo = split(pick_left(pick_ref[0], map1) + pick_ref[1].astype(F32))
+    zf_w[:, 0:LANES] = hi
+    zf_w[:, LANES:] = lo
+    place = turn_ref[0].astype(F32) + pick_right(map0, turn_ref[1])
+    for part, value in enumerate((place, wide(place, mf_w))):
+        hi, lo = split(value)
+        cols = slice(2 * LANES * part, 2 * LANES * (part + 1))
+        ze_w[0:LANES, cols] = hi
+        ze_w[LANES : 2 * LANES, cols] = hi
+        ze_w[2 * LANES :, cols] = lo
 
     fq, fv = coarse(jnp.zeros((ENV, LANES), F32), jnp.zeros((ENV, LANES), F32), True)
     free[:, 0:LANES] = fq
@@ -294,24 +308,21 @@
 
         def horizon(j, unused):
             def substep(counter, unused2):
-                for part in range(2):
-                    rows = slice(part * (ENV // 2), (part + 1) * (ENV // 2))
-                    q, v = q_ref[rows], v_ref[rows]
-                    n = (q + MAGIC) - MAGIC
-                    r = q - n
-                    r2 = r * r
-                    poly = coef[-1] * r2 + coef[-2]
-                    for value in coef[-3::-1]:
-                        poly = poly * r2 + value
-                    force = tau[j, rows] - kk[j, rows] * q - dd[j, rows] * v - r * poly
-                    hi, lo = split(force)
-                    out = dot(jnp.concatenate([hi, lo], axis=1), nfine[...])
-                    v = v + (out[:, 0:LANES] + out[:, LANES:])
-                    v_ref[rows] = v
-                    q_ref[rows] = q + v
+                q, v = q_ref[...], v_ref[...]
+                r = q - jnp.round(q)
+                r2 = r * r
+                r4 = r2 * r2
+                low, mid, high = (coef[i + 1] * r2 + coef[i] for i in (0, 2, 4))
+                poly = (high * r4 + mid) * r4 + low
+                force = tau[j] - kk[j] * q - dd[j] * v - r * poly
+                hi, lo = split(force)
+                out = dot(jnp.concatenate([hi, lo], axis=1), nfine[...])
+                v = v + (out[:, 0:LANES] + out[:, LANES:])
+                v_ref[...] = v
+                q_ref[...] = q + v
                 return unused2
 
-            return lax.fori_loop(0, SUB, substep, unused, unroll=4)
+            return lax.fori_loop(0, SUB, substep, unused, unroll=16)
 
         lax.fori_loop(0, 2, horizon, 0)
         free[:, 0:LANES] = q_ref[...] * TWO_PI
@@ -331,15 +342,17 @@
         corr[pl.ds(slot, 1), :] = largest[:, 0:LANES]
         corr[pl.ds(slot + 4, 1), :] = largest[:, LANES:]
 
-    def maps(part, unused):
+    def maps(offsets):
         rr = lax.broadcasted_iota(jnp.int32, (MROWS, LANES), 0)
         ll = lax.broadcasted_iota(jnp.int32, (MROWS, LANES), 1)
         base_q = ((rr == ll) & (ll < DOF)).astype(F32)
         base_v = ((rr == ll + DOF) & (ll < DOF)).astype(F32)
         keep = lane[0:1] < HALF
         one = [jnp.where(keep, par_ref[i : i + 1], 0.0) for i in range(5)]
-        for u in range(8):
-            p = part * 8 + u
+        for p, device in chips([dz for dz in offsets if dz]):
+            copy(n_buf, recv_n.at[p], sem_n.at[p], rsem_n.at[p], device).wait_recv()
+            copy(m_buf, recv_m.at[p], sem_m.at[p], rsem_m.at[p], device).wait_recv()
+        for u, (p, _) in enumerate(chips(offsets)):
             n_both = recv_n[p]
             means = recv_m[p]
             q, v = base_q, base_v
@@ -354,13 +367,21 @@
                     friction = one[1] + m * one[4]
                     v = v - DT * small(spring * q + friction * v, side_n[2 * u + s])
                     q = q + DT * v
-            full = q + pltpu.roll(v, DOF, 1)
-            prod[p] = full
-            put_side(side_a, p, full)
-        return unused
+            prod[p * NC + c] = q + pltpu.roll(v, DOF, 1)
+        for p, _ in chips(offsets):
+            swap(p * NC + c, p).start()
+
+    def swap(slot, p):
+        return copy(prod.at[slot], prod.at[slot], sem_p.at[p], rsem_p.at[p], {"c": 1 - c})
 
     def products():
-        lax.fori_loop(0, 2, maps, 0)
+        for offsets in NEAR_FIRST:
+            maps(offsets)
+        for p in range(NZ):
+            put_side(side_a, p * NC + c, prod[p * NC + c])
+        for p in range(NZ):
+            swap(p * NC + 1 - c, p).wait_recv()
+            put_side(side_a, p * NC + 1 - c, prod[p * NC + 1 - c])
         for i in range(4):
             acc = prod[4 * i]
             for j in range(1, 4):
@@ -389,7 +410,9 @@
             fine()
 
         fresh = free[...] - gee[...]
-        s_buf[...] = wide(fresh, zf_w)
+        hi, lo = split(fresh)
+        shifts = dot(hi, zf_w[...]) + dot(lo, zf_w[...])
+        s_buf[...] = shifts[:, 0:LANES] + shifts[:, LANES:]
         recv_s[k, me] = s_buf[pl.ds(me * BLOCK, BLOCK), :]
         s_copies = []
         for p, device in zc_peers():
@@ -403,13 +426,10 @@
         for part in range(2):
             cols = slice(part * LANES, (part + 1) * LANES)
             jshift[:, cols] = jnp.where(low, 0.0, pltpu.roll(fresh[:, cols], HALF, 1))
+        jshift[:, 2 * LANES :] = wide(jshift[:, 0 : 2 * LANES], mf_w)
 
         @pl.when(k == 0)
         def _():
-            for p, device in zc_peers():
-                copy(n_buf, recv_n.at[p], sem_n.at[p], rsem_n.at[p], device).wait_recv()
-            for p, device in zc_peers():
-                copy(m_buf, recv_m.at[p], sem_m.at[p], rsem_m.at[p], device).wait_recv()
             products()
 
         for p, device in zc_peers():
@@ -468,9 +488,10 @@
             copy(e_send.at[p], recv_e.at[k, p], sem_e.at[p], rsem_e.at[k, p], device).wait_recv()
 
         arrived = recv_e[k].reshape(ENV, LANES)
-        begin = wide(arrived, ze_w) + jshift[...]
-        start[...] = begin
-        gee[...] = wide(begin, mf_w)
+        hi, lo = split(arrived)
+        both = dot(jnp.concatenate([hi, lo], axis=1), ze_w[0 : 2 * LANES, :]) + dot(hi, ze_w[2 * LANES :, :])
+        start[...] = both[:, 0 : 2 * LANES] + jshift[:, 0 : 2 * LANES]
+        gee[...] = both[:, 2 * LANES :] + jshift[:, 2 * LANES :]
         for cp in s_copies:
             cp.wait_send()
         for cp in e_copies:
@@ -511,6 +532,8 @@
         best = jnp.maximum(best, recv_cx[p])
     corr_out_ref[:, 0:LANES] = best[0:ITERS]
     corr_out_ref[:, LANES:] = best[4 : 4 + ITERS]
+    for p in range(NZ):
+        swap(p * NC + c, p).wait_send()
     for cp in n_copies + m_copies + cz_copies + cx_copies:
         cp.wait_send()
     for k in range(1, NX):
@@ -549,17 +572,17 @@
         v(ENV, 2 * LANES),
         v(ENV, 2 * LANES),
         v(ENV, 2 * LANES),
-        v(ENV, 2 * LANES),
+        v(ENV, 4 * LANES),
         v(2, 2 * LANES, 2 * LANES, dtype=BF16),
-        v(2, 2 * LANES, LANES, dtype=BF16),
-        v(2, LANES, 2 * LANES, dtype=BF16),
+        v(2 * LANES, 2 * LANES, dtype=BF16),
+        v(3 * LANES, 4 * LANES, dtype=BF16),
         v(ENV, LANES),
         v(SWEEPS, GROUP, BLOCK, LANES),
         v(NROWS, LANES),
-        v(GROUP, NROWS, LANES),
+        v(NZ, NROWS, LANES),
         v(8, LANES),
-        v(GROUP, 8, LANES),
-        v(GROUP, LANES, 2 * LANES, dtype=BF16),
+        v(NZ, 8, LANES),
+        v(8, LANES, 2 * LANES, dtype=BF16),
         v(GROUP, LANES, 2 * LANES, dtype=BF16),
         v(4, LANES, 2 * LANES, dtype=BF16),
         v(GROUP, LANES, 2 * LANES, dtype=BF16),
@@ -580,8 +603,9 @@
         v(8, LANES),
         v(NX, 8, LANES),
         dma((NE,)), dma((NE,)),
-        dma((GROUP,)), dma((GROUP,)),
-        dma((GROUP,)), dma((GROUP,)),
+        dma((NZ,)), dma((NZ,)),
+        dma((NZ,)), dma((NZ,)),
+        dma((NZ,)), dma((NZ,)),
         dma((GROUP,)), dma((SWEEPS, GROUP)),
         dma((GROUP,)), dma((SWEEPS, GROUP)),
         dma((NX,)), dma((SWEEPS, NX)),

time: 130 us -> 117 us (0.900)
  Pallas kernels: 127 us -> 114 us
    pallas_call x1, Pallas kernels: 127 us -> 114 us  [shards(): pl.pallas_call(body, out_shape=(jax.ShapeDtypeStruct((STATE, 2, ENV), F32...]
where the time goes in v3:
time: 117 us
  Pallas kernels  114 us (97%)
  local copies, waits for them, and re-layouts  2.17 us (2%)
    pallas_call x1, Pallas kernels, shards(): pl.pallas_call(body, out_shape=(jax.ShapeDtypeStruct((STATE, 2, ENV), F32...  114 us

profile of v3, /device:TPU:1, one launch (start us, length us, event | category | flops | bytes accessed | tf_op | source)
XLA Modules:
  0.0 117.1 jit_solution(6415400667156597699)
XLA Ops:
  0.6 114.3 %parareal.1 = (f32[70,2,256]{2,1,0:T(2,128)}, f32[3,256]{1,0:T(4,128)}) custom-call(f32[70,256]{1,0:T(8,128)} %init_in.1, f32[35,4,256]{2,1,0:T(4,128)} %bitcast.8, s32[4,256]{1,0:T(4,128)} %contact_in.1, f32[35,2,35]{2,1,0:T(2,128)} %bitcast.10, f32[1,35]{1,0:T(1,128)} %bitcast.11, f32[1,35]{1,0:T(1,128)} %bitcast.12, f32[1,35]{1,0:T(1,128)} %bitcast.13, ...), custom_call_target="tpu_custom_call" | custom-call | tf_op jit(solution)/shard_map/parareal/pallas_call | solution.py:623
  115.0 0.0 copy-start
  115.0 1.6 %copy.15 = f32[2,70,256]{2,0,1:T(2,128)} copy(f32[2,70,256]{2,0,1:T(2,128)} %bitcast.9) | data formatting | bytes 286720
  116.6 0.0 copy-done
  116.6 0.6 copy.16
Async XLA Ops:
  115.0 1.6 %copy-start = (f32[3,256]{1,0:T(4,128)S(1)}, f32[3,256]{1,0:T(4,128)}, u32[]{:S(2)}) copy-start(f32[3,256]{1,0:T(4,128)} %get-tuple-element.9) | copy-start | bytes 9220

commit v4 on v3

--- a/solution.py
+++ b/solution.py
@@ -131,9 +131,9 @@
     init_in, torque_in, contact_in, minv_in, stiff_in, damp_in, grav_in, cstiff_in, cdamp_in, pick_in, turn_in,
     final_ref, corr_out_ref,
     init_ref, torque_ref, contact_ref, minv_ref, stiff_ref, damp_ref, grav_ref, cstiff_ref, cdamp_ref, pick_ref, turn_ref,
-    in_sem, par_ref, block_ref, flip, tau, kk, dd, q_ref, v_ref, init_t, nfine, free, jall, start, gee, ends, jshift,
+    in_sem, par_ref, block_ref, flip, tau, kk, dd, q_ref, v_ref, init_t, nfine, free, jall, start, gee, ends, jshift, map0_ref,
     mf_w, zf_w, ze_w, s_buf, recv_s, n_buf, recv_n, m_buf, recv_m, side_n, side_a, side_b, side_p, side_pp, side_c,
-    prod, ent, total_buf, recv_t, c_buf, recv_c, e_send, recv_e, cnt_buf, recv_cnt,
+    prod, lead_ref, ent, total_buf, recv_t, c_buf, recv_c, e_send, recv_e, cnt_buf, recv_cnt,
     corr, recv_cz, corr_x, recv_cx,
     sem_cnt, rsem_cnt, sem_n, rsem_n, sem_m, rsem_m, sem_p, rsem_p, sem_s, rsem_s, sem_e, rsem_e, sem_t, rsem_t, sem_c, rsem_c,
     sem_cz, rsem_cz, sem_cx, rsem_cx,
@@ -283,13 +283,7 @@
     hi, lo = split(pick_left(pick_ref[0], map1) + pick_ref[1].astype(F32))
     zf_w[:, 0:LANES] = hi
     zf_w[:, LANES:] = lo
-    place = turn_ref[0].astype(F32) + pick_right(map0, turn_ref[1])
-    for part, value in enumerate((place, wide(place, mf_w))):
-        hi, lo = split(value)
-        cols = slice(2 * LANES * part, 2 * LANES * (part + 1))
-        ze_w[0:LANES, cols] = hi
-        ze_w[LANES : 2 * LANES, cols] = hi
-        ze_w[2 * LANES :, cols] = lo
+    map0_ref[...] = map0
 
     fq, fv = coarse(jnp.zeros((ENV, LANES), F32), jnp.zeros((ENV, LANES), F32), True)
     free[:, 0:LANES] = fq
@@ -322,7 +316,7 @@
                 q_ref[...] = q + v
                 return unused2
 
-            return lax.fori_loop(0, SUB, substep, unused, unroll=16)
+            return lax.fori_loop(0, SUB, substep, unused, unroll=32)
 
         lax.fori_loop(0, 2, horizon, 0)
         free[:, 0:LANES] = q_ref[...] * TWO_PI
@@ -333,12 +327,14 @@
         change = new - ends[...]
         ends[...] = new
         square = change * change
-        lanes2 = lax.broadcasted_iota(jnp.int32, (8, LANES), 1)
-        first = (lanes2 < HALF).astype(F32)
         folded = square[:, 0:LANES] + square[:, LANES:]
-        sum0 = exact_tb(first, folded)
-        sum1 = exact_tb(1.0 - first, folded)
-        largest = jnp.sqrt(jnp.maximum(sum0, sum1))[0:1]
+        ones = ((row == 0) & (lane < HALF)) | ((row == 1) & (lane >= HALF))
+        ones = ones.astype(F32).astype(BF16)
+        sums = None
+        for piece in split(folded):
+            term = lax.dot_general(ones, piece, (((1,), (1,)), ((), ())), preferred_element_type=F32)
+            sums = term if sums is None else sums + term
+        largest = jnp.sqrt(jnp.maximum(sums[0:1], sums[1:2]))
         corr[pl.ds(slot, 1), :] = largest[:, 0:LANES]
         corr[pl.ds(slot + 4, 1), :] = largest[:, LANES:]
 
@@ -388,21 +384,40 @@
                 put_side(side_p, 4 * i + j, acc)
                 acc = small(acc, side_a[4 * i + j])
             put_side(side_b, i, acc)
+            lead_ref[i] = acc
             if i == 0:
                 before = acc
+        leads = [before]
+        for i in range(1, 4):
+            leads.append(small(leads[-1], side_b[i]))
+        c_buf[...] = leads[3]
+        for k in range(1, NX):
+
+            @pl.when(x + k < NX)
+            def _():
+                copy(c_buf, recv_c.at[x], sem_c.at[k], rsem_c.at[x], {"x": lax.rem(x + k, NX)}).start()
+
+        two = small(lead_ref[1], side_b[2])
+        put_side(side_b, 4, two)
+        put_side(side_b, 5, small(lead_ref[2], side_b[3]))
+        put_side(side_b, 6, small(two, side_b[3]))
+        for i in range(3):
+            lead_ref[i] = leads[i]
         for j in range(1, 4):
             side_pp[j] = side_p[j]
         for i in range(1, 4):
-            put_side(side_pp, 4 * i, before)
+            put_side(side_pp, 4 * i, lead_ref[i - 1])
             for j in range(1, 4):
-                put_side(side_pp, 4 * i + j, small(before, side_p[4 * i + j]))
-            before = small(before, side_b[i])
-        c_buf[...] = before
-        for k in range(1, NX):
-
-            @pl.when(x + k < NX)
-            def _():
-                copy(c_buf, recv_c.at[x], sem_c.at[k], rsem_c.at[x], {"x": lax.rem(x + k, NX)}).start()
+                put_side(side_pp, 4 * i + j, small(lead_ref[i - 1], side_p[4 * i + j]))
+
+    def place_maps():
+        place = turn_ref[0].astype(F32) + pick_right(map0_ref[...], turn_ref[1])
+        for part, value in enumerate((place, wide(place, mf_w))):
+            hi, lo = split(value)
+            cols = slice(2 * LANES * part, 2 * LANES * (part + 1))
+            ze_w[0:LANES, cols] = hi
+            ze_w[LANES : 2 * LANES, cols] = hi
+            ze_w[2 * LANES :, cols] = lo
 
     def sweep(k, unused):
         @pl.when(k > 0)
@@ -420,13 +435,11 @@
             cp.start()
             s_copies.append(cp)
 
-        settle(lax.max(k - 2, 0))
+        @pl.when(k > 0)
+        def _():
+            settle(lax.max(k - 2, 0))
+
         jall[...] = fresh
-        low = lax.broadcasted_iota(jnp.int32, (ENV, LANES), 1) < HALF
-        for part in range(2):
-            cols = slice(part * LANES, (part + 1) * LANES)
-            jshift[:, cols] = jnp.where(low, 0.0, pltpu.roll(fresh[:, cols], HALF, 1))
-        jshift[:, 2 * LANES :] = wide(jshift[:, 0 : 2 * LANES], mf_w)
 
         @pl.when(k == 0)
         def _():
@@ -443,16 +456,21 @@
                 inside[i, j] = acc
                 acc = small(acc, side_a[4 * i + j]) + recv_s[k, 4 * i + j]
             totals.append(acc)
-        entry = [None, totals[0]]
-        for i in range(1, 4):
-            entry.append(small(entry[i], side_b[i]) + totals[i])
-        total_buf[...] = entry[4]
+        total_buf[...] = (
+            small(totals[0], side_b[6]) + small(totals[1], side_b[5]) + small(totals[2], side_b[3]) + totals[3]
+        )
         for d in range(1, NX):
 
             @pl.when(x + d < NX)
             def _():
                 copy(total_buf, recv_t.at[k, x], sem_t.at[d], rsem_t.at[k, x], {"x": lax.rem(x + d, NX)}).start()
 
+        entry = [
+            None,
+            totals[0],
+            small(totals[0], side_b[1]) + totals[1],
+            small(totals[0], side_b[4]) + small(totals[1], side_b[2]) + totals[2],
+        ]
         for i in range(4):
             if i > 0:
                 ent[4 * i] = entry[i]
@@ -484,6 +502,16 @@
             cp = copy(e_send.at[p], recv_e.at[k, me], sem_e.at[p], rsem_e.at[k, me], device)
             cp.start()
             e_copies.append(cp)
+
+        @pl.when(k == 0)
+        def _():
+            place_maps()
+
+        low = lax.broadcasted_iota(jnp.int32, (ENV, LANES), 1) < HALF
+        for part in range(2):
+            cols = slice(part * LANES, (part + 1) * LANES)
+            jshift[:, cols] = jnp.where(low, 0.0, pltpu.roll(jall[:, cols], HALF, 1))
+        jshift[:, 2 * LANES :] = wide(jshift[:, 0 : 2 * LANES], mf_w)
         for p, device in zc_peers():
             copy(e_send.at[p], recv_e.at[k, p], sem_e.at[p], rsem_e.at[k, p], device).wait_recv()
 
@@ -573,6 +601,7 @@
         v(ENV, 2 * LANES),
         v(ENV, 2 * LANES),
         v(ENV, 4 * LANES),
+        v(LANES, LANES),
         v(2, 2 * LANES, 2 * LANES, dtype=BF16),
         v(2 * LANES, 2 * LANES, dtype=BF16),
         v(3 * LANES, 4 * LANES, dtype=BF16),
@@ -584,11 +613,12 @@
         v(NZ, 8, LANES),
         v(8, LANES, 2 * LANES, dtype=BF16),
         v(GROUP, LANES, 2 * LANES, dtype=BF16),
-        v(4, LANES, 2 * LANES, dtype=BF16),
+        v(7, LANES, 2 * LANES, dtype=BF16),
         v(GROUP, LANES, 2 * LANES, dtype=BF16),
         v(GROUP, LANES, 2 * LANES, dtype=BF16),
         v(NX, LANES, 2 * LANES, dtype=BF16),
         v(GROUP, MROWS, LANES),
+        v(4, MROWS, LANES),
         v(GROUP, BLOCK, LANES),
         v(BLOCK, LANES),
         v(SWEEPS, NX, BLOCK, LANES),

time: 117 us -> 116 us (level)
    pallas_call x1, Pallas kernels: 114 us -> 113 us  [shards(): pl.pallas_call(body, out_shape=(jax.ShapeDtypeStruct((STATE, 2, ENV), F32...]
where the time goes in v4:
time: 116 us; the launch traced here: 115 us
  Pallas kernels  113 us (97%)
  local copies, waits for them, and re-layouts  2.17 us (2%)
    pallas_call x1, Pallas kernels, shards(): pl.pallas_call(body, out_shape=(jax.ShapeDtypeStruct((STATE, 2, ENV), F32...  113 us

profile of v4, /device:TPU:1, one launch (start us, length us, event | category | flops | bytes accessed | tf_op | source)
XLA Modules:
  0.0 115.4 jit_solution(12633087296656289617)
XLA Ops:
  0.6 112.6 %parareal.1 = (f32[70,2,256]{2,1,0:T(2,128)}, f32[3,256]{1,0:T(4,128)}) custom-call(f32[70,256]{1,0:T(8,128)} %init_in.1, f32[35,4,256]{2,1,0:T(4,128)} %bitcast.8, s32[4,256]{1,0:T(4,128)} %contact_in.1, f32[35,2,35]{2,1,0:T(2,128)} %bitcast.10, f32[1,35]{1,0:T(1,128)} %bitcast.11, f32[1,35]{1,0:T(1,128)} %bitcast.12, f32[1,35]{1,0:T(1,128)} %bitcast.13, ...), custom_call_target="tpu_custom_call" | custom-call | tf_op jit(solution)/shard_map/parareal/pallas_call | solution.py:653
  113.2 0.0 copy-start
  113.2 1.6 %copy.15 = f32[2,70,256]{2,0,1:T(2,128)} copy(f32[2,70,256]{2,0,1:T(2,128)} %bitcast.9) | data formatting | bytes 286720
  114.8 0.0 copy-done
  114.8 0.6 copy.16
Async XLA Ops:
  113.2 1.6 %copy-start = (f32[3,256]{1,0:T(4,128)S(1)}, f32[3,256]{1,0:T(4,128)}, u32[]{:S(2)}) copy-start(f32[3,256]{1,0:T(4,128)} %get-tuple-element.9) | copy-start | bytes 9220

commit v5 on v4

--- a/solution.py
+++ b/solution.py
@@ -419,6 +419,16 @@
             ze_w[LANES : 2 * LANES, cols] = hi
             ze_w[2 * LANES :, cols] = lo
 
+    def sent(k):
+        for p, device in zc_peers():
+            copy(e_send.at[p], recv_e.at[k - 1, me], sem_e.at[p], rsem_e.at[k - 1, me], device).wait_send()
+        for d in range(1, NX):
+
+            @pl.when(x + d < NX)
+            def _():
+                device = {"x": lax.rem(x + d, NX)}
+                copy(total_buf, recv_t.at[k - 1, x], sem_t.at[d], rsem_t.at[k - 1, x], device).wait_send()
+
     def sweep(k, unused):
         @pl.when(k > 0)
         def _():
@@ -437,6 +447,7 @@
 
         @pl.when(k > 0)
         def _():
+            sent(k)
             settle(lax.max(k - 2, 0))
 
         jall[...] = fresh
@@ -497,11 +508,10 @@
         for d in range(1, GROUP):
             e_send[d] = small(first, side_pp[d]) + ent[d]
         recv_e[k, me] = e_send[me]
-        e_copies = []
         for p, device in zc_peers():
-            cp = copy(e_send.at[p], recv_e.at[k, me], sem_e.at[p], rsem_e.at[k, me], device)
-            cp.start()
-            e_copies.append(cp)
+            copy(e_send.at[p], recv_e.at[k, me], sem_e.at[p], rsem_e.at[k, me], device).start()
+        for cp in s_copies:
+            cp.wait_send()
 
         @pl.when(k == 0)
         def _():
@@ -520,16 +530,6 @@
         both = dot(jnp.concatenate([hi, lo], axis=1), ze_w[0 : 2 * LANES, :]) + dot(hi, ze_w[2 * LANES :, :])
         start[...] = both[:, 0 : 2 * LANES] + jshift[:, 0 : 2 * LANES]
         gee[...] = both[:, 2 * LANES :] + jshift[:, 2 * LANES :]
-        for cp in s_copies:
-            cp.wait_send()
-        for cp in e_copies:
-            cp.wait_send()
-        for d in range(1, NX):
-
-            @pl.when(x + d < NX)
-            def _():
-                copy(total_buf, recv_t.at[k, x], sem_t.at[d], rsem_t.at[k, x], {"x": lax.rem(x + d, NX)}).wait_send()
-
         return unused
 
     lax.fori_loop(0, SWEEPS, sweep, 0)
@@ -545,6 +545,7 @@
         final_ref[:, s, :] = lax.dot_general(
             pick_ref[s].astype(F32), ends[...], (((0,), (1,)), ((), ())), precision=HIGHEST, preferred_element_type=F32
         )[0:STATE]
+    sent(SWEEPS)
     for p, device in zc_peers():
         copy(corr, recv_cz.at[p], sem_cz.at[p], rsem_cz.at[p], device).wait_recv()
     corr_x[...] = jnp.max(recv_cz[...], axis=0)

time: 116 us -> 115 us (level)
  no operation moved by 1% of the time
where the time goes in v5:
time: 115 us
  Pallas kernels  112 us (97%)
  local copies, waits for them, and re-layouts  2.17 us (2%)
    pallas_call x1, Pallas kernels, shards(): pl.pallas_call(body, out_shape=(jax.ShapeDtypeStruct((STATE, 2, ENV), F32...  112 us

profile of v5, /device:TPU:1, one launch (start us, length us, event | category | flops | bytes accessed | tf_op | source)
XLA Modules:
  0.0 114.8 jit_solution(6165487092178222638)
XLA Ops:
  0.6 111.9 %parareal.1 = (f32[70,2,256]{2,1,0:T(2,128)}, f32[3,256]{1,0:T(4,128)}) custom-call(f32[70,256]{1,0:T(8,128)} %init_in.1, f32[35,4,256]{2,1,0:T(4,128)} %bitcast.8, s32[4,256]{1,0:T(4,128)} %contact_in.1, f32[35,2,35]{2,1,0:T(2,128)} %bitcast.10, f32[1,35]{1,0:T(1,128)} %bitcast.11, f32[1,35]{1,0:T(1,128)} %bitcast.12, f32[1,35]{1,0:T(1,128)} %bitcast.13, ...), custom_call_target="tpu_custom_call" | custom-call | tf_op jit(solution)/shard_map/parareal/pallas_call | solution.py:654
  112.6 0.0 copy-start
  112.6 1.6 %copy.15 = f32[2,70,256]{2,0,1:T(2,128)} copy(f32[2,70,256]{2,0,1:T(2,128)} %bitcast.9) | data formatting | bytes 286720
  114.2 0.0 copy-done
  114.2 0.6 copy.16
Async XLA Ops:
  112.6 1.6 %copy-start = (f32[3,256]{1,0:T(4,128)S(1)}, f32[3,256]{1,0:T(4,128)}, u32[]{:S(2)}) copy-start(f32[3,256]{1,0:T(4,128)} %get-tuple-element.9) | copy-start | bytes 9220
